TPU v7x, 256 devices: a whole 4x4x8 slice. The times are simulated.
256 devices in a mesh: dp: 16 (over x, y_hi, core), pencil: 16 (over z, y_lo).
Axes of the slice: x: 4, y: 4 (y_hi: 2, y_lo: 2; y = y_hi * 2 + y_lo), z: 8, core: 2. Of those that a mesh axis runs over, the one named last changes fastest.
Arguments:
- field: bfloat16 [16, 64, 64, 64, 128], P('dp', 'pencil'), may hold values from -6 to 6
- cotangent: bfloat16 [16, 64, 64, 64, 128], P('dp', 'pencil'), may hold values from -6 to 6
- w_spec: bfloat16 [16, 16, 16, 64, 128], P('dp', 'pencil'), may hold values from -6 to 6
- w_local: bfloat16 [64, 64], replicated, may hold values from -0.75 to 0.75
Outputs:
- grad_field: bfloat16 [16, 64, 64, 64, 128], P('dp', 'pencil')
- grad_w: float32 [16, 16, 16, 64, 128], P('dp', 'pencil')
All inputs are finite; a program needn't handle non-finite values.
Results may differ from a plain program's by a relative error of at most 0.02.
Values may be sent and summed in bfloat16 or wider, within the bound.
A program may use at most 128 MiB of HBM per device.

v0:
```python
import math

import jax
import jax.numpy as jnp
from jax import lax
from jax.sharding import PartitionSpec as P

NX = 64
NY = 64
NZ = 128
CH = 64
MX = 16
MY = 16
MZ = 16


def phase_pair(length, mode_count, signed):
    position = jnp.arange(length, dtype=jnp.int32)
    indices = jnp.arange(mode_count, dtype=jnp.int32)
    frequency = (
        jnp.where(indices < mode_count // 2, indices, indices - mode_count) if signed else indices
    )
    product = jnp.mod(position[:, None] * frequency[None, :], length).astype(jnp.float32)
    angles = product * (2.0 * math.pi / length)
    return (jnp.cos(angles), jnp.sin(angles))


def grid_tables():
    cos_x, sin_x = phase_pair(NX, MX, True)
    cos_y, sin_y = phase_pair(NY, MY, True)
    cos_z, sin_z = phase_pair(NZ, MZ, False)
    forward_z = jnp.concatenate([cos_z, -sin_z], 1).astype(jnp.bfloat16)
    weight_z = jnp.where(jnp.arange(MZ, dtype=jnp.int32) == 0, 1.0, 2.0).astype(jnp.float32) / (
        NX * NY * NZ
    )
    inverse_z = jnp.concatenate([cos_z * weight_z, -sin_z * weight_z], 1).T
    adjoint_z = jnp.concatenate([cos_z, -sin_z], 1).T
    spectrum_scale = jnp.concatenate([weight_z, weight_z])
    return (cos_x, sin_x, cos_y, sin_y, forward_z, inverse_z, adjoint_z, spectrum_scale)


def rotate_half(values):
    middle = values.shape[-1] // 2
    return jnp.concatenate([values[..., middle:], -values[..., :middle]], -1)


def along_y(values, cosines, sine_table, inverse):
    pattern = "xjck,yj->xyck" if inverse else "xyck,yj->xjck"
    factor = -1.0 if inverse else 1.0
    direct = jnp.einsum(pattern, values, cosines)
    turned = jnp.einsum(pattern, rotate_half(values), sine_table)
    return direct + factor * turned


def along_x(values, cosines, sine_table, inverse):
    pattern = "jbck,xj->xbck" if inverse else "xbck,xj->jbck"
    factor = -1.0 if inverse else 1.0
    direct = jnp.einsum(pattern, values, cosines)
    turned = jnp.einsum(pattern, rotate_half(values), sine_table)
    return direct + factor * turned


def z_forward(field_in, matrix):
    shape_in = field_in.shape
    product = jnp.dot(
        field_in.reshape(-1, shape_in[-1]), matrix, preferred_element_type=jnp.float32
    )
    return product.reshape(shape_in[:-1] + (matrix.shape[1],))


def z_back(values, matrix):
    shape_in = values.shape
    product = jnp.dot(values.reshape(-1, shape_in[-1]), matrix, preferred_element_type=jnp.float32)
    return product.reshape(shape_in[:-1] + (matrix.shape[1],))


def gelu_slope(pre):
    normal_cdf = 0.5 * (1.0 + lax.erf(pre * (1.0 / math.sqrt(2.0))))
    return normal_cdf + pre * jnp.exp(-0.5 * pre * pre) * (1.0 / math.sqrt(2.0 * math.pi))


def apply_modes(coeffs, weights):
    real_part = coeffs[..., :MZ]
    imag_part = coeffs[..., MZ:]
    from_real = jnp.einsum(
        "sabik,abkio->sabok", real_part, weights, preferred_element_type=jnp.float32
    )
    from_imag = jnp.einsum(
        "sabik,abkio->sabok", imag_part, weights, preferred_element_type=jnp.float32
    )
    out_real = from_real[:, :, :, :CH] - from_imag[:, :, :, CH:]
    out_imag = from_real[:, :, :, CH:] + from_imag[:, :, :, :CH]
    return jnp.concatenate([out_real, out_imag], -1)


def paired(g_modes):
    g_real = g_modes[..., :MZ]
    g_imag = g_modes[..., MZ:]
    return (jnp.concatenate([g_real, g_imag], -2), jnp.concatenate([g_imag, -g_real], -2))


def adjoint_modes(g_modes, weights):
    paired_one, paired_two = paired(g_modes)
    back_real = jnp.einsum(
        "abkio,sabok->sabik", weights, paired_one, preferred_element_type=jnp.float32
    )
    back_imag = jnp.einsum(
        "abkio,sabok->sabik", weights, paired_two, preferred_element_type=jnp.float32
    )
    return jnp.concatenate([back_real, back_imag], -1)


def mode_grads(u_modes, g_modes):
    paired_one, paired_two = paired(g_modes)
    from_real = jnp.einsum(
        "sabik,sabok->abkio", u_modes[..., :MZ], paired_one, preferred_element_type=jnp.float32
    )
    from_imag = jnp.einsum(
        "sabik,sabok->abkio", u_modes[..., MZ:], paired_two, preferred_element_type=jnp.float32
    )
    return from_real + from_imag


def to_modes(field_in, tables):
    cos_x, sin_x, cos_y, sin_y, forward_z = (tables[0], tables[1], tables[2], tables[3], tables[4])
    sectioned = along_y(z_forward(field_in, forward_z), cos_y, sin_y, False)
    arrived = lax.all_to_all(
        sectioned.astype(jnp.bfloat16), "pencil", split_axis=1, concat_axis=0, tiled=True
    ).astype(sectioned.dtype)
    return along_x(arrived, cos_x, sin_x, False)


def to_grid(coeffs, tables, matrix):
    cos_x, sin_x, cos_y, sin_y = (tables[0], tables[1], tables[2], tables[3])
    sectioned = along_x(coeffs, cos_x, sin_x, True)
    arrived = lax.all_to_all(
        sectioned.astype(jnp.bfloat16), "pencil", split_axis=0, concat_axis=1, tiled=True
    ).astype(sectioned.dtype)
    return z_back(along_y(arrived, cos_y, sin_y, True), matrix)


def to_owner(coeffs):
    return lax.all_to_all(coeffs[None], "dp", split_axis=1, concat_axis=0, tiled=True)


def from_owner(coeffs):
    return lax.all_to_all(
        coeffs.astype(jnp.bfloat16), "dp", split_axis=0, concat_axis=1, tiled=True
    ).astype(coeffs.dtype)[0]


def body(field, cotangent, w_spec, w_local):
    tables = grid_tables()
    inverse_z, adjoint_z, spectrum_scale = (tables[5], tables[6], tables[7])
    sample = field[0]
    target = cotangent[0]
    u_modes = to_modes(sample, tables).astype(jnp.bfloat16)
    u_sent = to_owner(u_modes)
    v_modes = from_owner(apply_modes(u_sent, w_spec))
    values = to_grid(v_modes, tables, inverse_z)
    bypass = jnp.einsum("xycz,co->xyoz", sample, w_local, preferred_element_type=jnp.float32)
    slope_in = (target.astype(jnp.float32) * gelu_slope(values + bypass)).astype(jnp.bfloat16)
    g_modes = (to_modes(slope_in, tables) * spectrum_scale).astype(jnp.bfloat16)
    g_sent = to_owner(g_modes)
    grad_w = mode_grads(u_sent, g_sent)
    back_modes = from_owner(adjoint_modes(g_sent, w_spec))
    spread = jnp.einsum("xyoz,co->xycz", slope_in, w_local, preferred_element_type=jnp.float32)
    grad_sample = (to_grid(back_modes, tables, adjoint_z) + spread).astype(jnp.bfloat16)
    return (grad_sample[None], grad_w)


def solution(mesh):
    placed = (
        P("dp", "pencil", None, None, None),
        P("dp", "pencil", None, None, None),
        P("dp", "pencil", None, None, None),
        P(),
    )
    return jax.shard_map(
        body,
        mesh=mesh,
        in_specs=placed,
        out_specs=(P("dp", "pencil", None, None, None), P("dp", "pencil", None, None, None)),
        check_vma=False,
    )
```

profile of v0, /device:TPU:8, one launch (start us, length us, event | category | flops | bytes accessed | tf_op | source)
XLA Modules:
  0.0 166.1 jit_solution(9578072925121026040)
XLA Ops:
  0.7 3.7 %convolution_bitcast_fusion = f32[16384,32]{0,1:T(8,128)S(1)} fusion(bf16[16384,128]{1,0:T(8,128)(2,1)} %bitcast.246, bf16[128,16]{0,1:T(8,128)(2,1)S(1)} %get-tuple-element.21, bf16[128,16]{0,1:T(8,128)(2,1)S(1)} %get-tuple-element.22), kind=kOutput, calls=%fused_computation | convolution fusion | flops 134234112 | bytes 6299648 | tf_op jit(solution)/shard_map/dot_general | solution.py:65
  4.4 3.0 %reshape.248 = f32[4,64,64,32]{2,1,0,3:T(8,128)} reshape(f32[16384,32]{0,1:T(8,128)S(1)} %convolution_bitcast_fusion) | data formatting | bytes 4194304 | tf_op jit(solution)/shard_map/reshape | solution.py:68
  7.5 3.0 %fusion.229 = (bf16[4,64,64,16]{2,1,3,0:T(8,128)(2,1)S(1)}, bf16[4,64,64,16]{2,1,3,0:T(8,128)(2,1)S(1)}) fusion(f32[4,64,64,32]{2,1,0,3:T(8,128)} %reshape.248), kind=kLoop, calls=%fused_computation.258 | loop fusion | flops 524288 | bytes 4194304 | tf_op jit(solution)/shard_map/slice | solution.py:44
  12.6 20.2 %all_to_all.108 = bf16[16,2,4096]{2,1,0:T(2,128)(2,1)S(1)} all-to-all(bf16[16,2,4096]{2,1,0:T(2,128)(2,1)S(1)} %reshape.276), channel_id=1, replica_groups=mesh['dp'=16,'pencil'=16] {'pencil'}, dimensions={0} | all-to-all | bytes 524288 | tf_op jit(solution)/shard_map/all_to_all | solution.py:127
  35.2 6.1 %all-to-all-start.1 = ((bf16[16,2,1024]{2,1,0:T(2,128)(2,1)}), bf16[16,2,1024]{2,1,0:T(2,128)(2,1)S(1)}, u32[]{:S(2)}, u32[]{:S(2)}) async-start(bf16[16,2,1024]{2,1,0:T(2,128)(2,1)} %reshape.278), calls=%async_computation.1 | async-start | bytes 131072 | tf_op jit(solution)/shard_map/all_to_all | solution.py:143
  41.3 7.7 %all-to-all-done.1 = bf16[16,2,1024]{2,1,0:T(2,128)(2,1)S(1)} async-done(((bf16[16,2,1024]{2,1,0:T(2,128)(2,1)}), bf16[16,2,1024]{2,1,0:T(2,128)(2,1)S(1)}, u32[]{:S(2)}, u32[]{:S(2)}) %all-to-all-start.1) | async-done | bytes 65568 | tf_op jit(solution)/shard_map/all_to_all | solution.py:143
  50.6 3.5 %all-to-all-start.2 = ((bf16[16,2,1024]{2,1,0:T(2,128)(2,1)}), bf16[16,2,1024]{2,1,0:T(2,128)(2,1)S(1)}, u32[]{:S(2)}, u32[]{:S(2)}) async-start(bf16[16,2,1024]{2,1,0:T(2,128)(2,1)} %reshape.280), calls=%async_computation.2 | async-start | bytes 131072 | tf_op jit(solution)/shard_map/all_to_all | solution.py:147
  54.2 7.5 %all-to-all-done.2 = bf16[16,2,1024]{2,1,0:T(2,128)(2,1)S(1)} async-done(((bf16[16,2,1024]{2,1,0:T(2,128)(2,1)}), bf16[16,2,1024]{2,1,0:T(2,128)(2,1)S(1)}, u32[]{:S(2)}, u32[]{:S(2)}) %all-to-all-start.2) | async-done | bytes 65568 | tf_op jit(solution)/shard_map/all_to_all | solution.py:147
  63.2 1.1 reshape.282
  64.3 5.5 %all-to-all-start.3 = ((bf16[16,2,4096]{2,1,0:T(2,128)(2,1)}), bf16[16,2,4096]{2,1,0:T(2,128)(2,1)S(1)}, u32[]{:S(2)}, u32[]{:S(2)}) async-start(bf16[16,2,4096]{2,1,0:T(2,128)(2,1)} %reshape.282), calls=%async_computation.3 | async-start | bytes 524288 | tf_op jit(solution)/shard_map/all_to_all | solution.py:136
  69.8 6.7 %fusion.12 = f32[64,4,64,128]{3,0,2,1:T(8,128)} fusion(bf16[1,4,64,64,128]{4,3,2,1,0:T(8,128)(2,1)} %param.4, bf16[64,64]{1,0:T(8,128)(2,1)S(1)} %copy-done.5), kind=kOutput, calls=%fused_computation.17 | convolution fusion | flops 268435456 | bytes 12591104 | tf_op jit(solution)/shard_map/xycz,co->xyoz/dot_general | solution.py:161
  76.5 5.0 %all-to-all-done.3 = bf16[16,2,4096]{2,1,0:T(2,128)(2,1)S(1)} async-done(((bf16[16,2,4096]{2,1,0:T(2,128)(2,1)}), bf16[16,2,4096]{2,1,0:T(2,128)(2,1)S(1)}, u32[]{:S(2)}, u32[]{:S(2)}) %all-to-all-start.3) | async-done | bytes 262176 | tf_op jit(solution)/shard_map/all_to_all | solution.py:136
  81.9 0.9 fusion.68
  83.2 0.9 add_bitcast_fusion.1
  84.1 2.7 %copy-done.4 = f32[64,4,64,128]{3,0,2,1:T(8,128)S(1)} copy-done((f32[64,4,64,128]{3,0,2,1:T(8,128)S(1)}, f32[64,4,64,128]{3,0,2,1:T(8,128)}, u32[]{:S(2)}) %copy-start.4) | copy-done | bytes 8388632
  86.8 5.5 %fusion.5 = bf16[4,64,64,128]{3,2,1,0:T(8,128)(2,1)S(1)} fusion(f32[64,4,64,128]{3,0,2,1:T(8,128)S(1)} %copy-done.4, bf16[1,4,64,64,128]{4,3,2,1,0:T(8,128)(2,1)S(1)} %copy-done.6, bf16[4,64,64,32]{2,1,3,0:T(8,128)(2,1)S(1)} %add_bitcast_fusion.1, bf16[128,16]{0,1:T(8,128)(2,1)S(1)} %get-tuple-element.20, bf16[128,16]{0,1:T(8,128)(2,1)S(1)} %get-tuple-element.19), kind=kOutput, calls=%fused_computation.7 | convolution fusion | flops 159399936 | bytes 17833984 | tf_op jit(solution)/shard_map/dot_general | solution.py:73
  92.3 4.0 %fusion.101 = f32[4,64,64,32]{2,3,1,0:T(8,128)S(1)} fusion(bf16[4,64,64,128]{3,2,1,0:T(8,128)(2,1)S(1)} %fusion.5, bf16[128,16]{0,1:T(8,128)(2,1)S(1)} %get-tuple-element.21, bf16[128,16]{0,1:T(8,128)(2,1)S(1)} %get-tuple-element.22), kind=kOutput, calls=%fused_computation.141 | convolution fusion | flops 134234112 | bytes 6299648 | tf_op jit(solution)/shard_map/dot_general | solution.py:65
  97.1 0.8 fusion.16
  97.8 2.4 %fusion.41 = bf16[4,16,64,32]{2,1,3,0:T(8,128)(2,1)S(1)} fusion(f32[16,4,64,32]{2,0,3,1:T(8,128)S(1)} %fusion.16, f32[4,64,64,32]{2,3,1,0:T(8,128)S(1)} %fusion.101, s32[16]{0:T(128)S(1)} %compare_select_fusion), kind=kOutput, calls=%fused_computation.45 | convolution fusion | flops 17053696 | bytes 2883648 | tf_op jit(solution)/shard_map/xyck,yj->xjck/dot_general | solution.py:50
  100.4 1.1 reshape.284
  101.5 4.8 %all-to-all-start.4 = ((bf16[16,2,4096]{2,1,0:T(2,128)(2,1)}), bf16[16,2,4096]{2,1,0:T(2,128)(2,1)S(1)}, u32[]{:S(2)}, u32[]{:S(2)}) async-start(bf16[16,2,4096]{2,1,0:T(2,128)(2,1)} %reshape.284), calls=%async_computation.4 | async-start | bytes 524288 | tf_op jit(solution)/shard_map/all_to_all | solution.py:127
  106.4 9.6 %all-to-all-done.4 = bf16[16,2,4096]{2,1,0:T(2,128)(2,1)S(1)} async-done(((bf16[16,2,4096]{2,1,0:T(2,128)(2,1)}), bf16[16,2,4096]{2,1,0:T(2,128)(2,1)S(1)}, u32[]{:S(2)}, u32[]{:S(2)}) %all-to-all-start.4) | async-done | bytes 262176 | tf_op jit(solution)/shard_map/all_to_all | solution.py:127
  117.7 10.2 %all_to_all.109 = bf16[16,2,1024]{2,1,0:T(2,128)(2,1)S(1)} all-to-all(bf16[16,2,1024]{2,1,0:T(2,128)(2,1)S(1)} %reshape.286), channel_id=1, replica_groups=mesh['dp'=16,'pencil'=16] {'dp'}, dimensions={0} | all-to-all | bytes 131072 | tf_op jit(solution)/shard_map/all_to_all | solution.py:143
  129.0 10.2 %all_to_all.110 = bf16[16,2,1024]{2,1,0:T(2,128)(2,1)S(1)} all-to-all(bf16[16,2,1024]{2,1,0:T(2,128)(2,1)S(1)} %reshape.288), channel_id=1, replica_groups=mesh['dp'=16,'pencil'=16] {'dp'}, dimensions={0} | all-to-all | bytes 131072 | tf_op jit(solution)/shard_map/all_to_all | solution.py:147
  140.7 1.1 reshape.290
  141.8 5.2 %all-to-all-start.7 = ((bf16[16,2,4096]{2,1,0:T(2,128)(2,1)}), bf16[16,2,4096]{2,1,0:T(2,128)(2,1)S(1)}, u32[]{:S(2)}, u32[]{:S(2)}) async-start(bf16[16,2,4096]{2,1,0:T(2,128)(2,1)} %reshape.290), calls=%async_computation.7 | async-start | bytes 524288 | tf_op jit(solution)/shard_map/all_to_all | solution.py:136
  147.3 1.1 fusion.40
  148.4 9.7 %all-to-all-done.7 = bf16[16,2,4096]{2,1,0:T(2,128)(2,1)S(1)} async-done(((bf16[16,2,4096]{2,1,0:T(2,128)(2,1)}), bf16[16,2,4096]{2,1,0:T(2,128)(2,1)S(1)}, u32[]{:S(2)}, u32[]{:S(2)}) %all-to-all-start.7) | async-done | bytes 262176 | tf_op jit(solution)/shard_map/all_to_all | solution.py:136
  158.5 0.9 fusion.66
  159.7 0.8 add_bitcast_fusion
  160.6 2.2 %fusion.14 = f32[4,64,64,128]{3,2,1,0:T(8,128)S(1)} fusion(bf16[4,64,64,32]{2,1,3,0:T(8,128)(2,1)S(1)} %add_bitcast_fusion, bf16[128,16]{0,1:T(8,128)(2,1)S(1)} %get-tuple-element.21, bf16[128,16]{0,1:T(8,128)(2,1)S(1)} %get-tuple-element.22), kind=kOutput, calls=%fused_computation.19 | convolution fusion | flops 134234112 | bytes 9445376 | tf_op jit(solution)/shard_map/dot_general | solution.py:73
  162.8 3.2 %fusion.7 = bf16[1,4,64,64,128]{4,3,2,1,0:T(8,128)(2,1)} fusion(f32[4,64,64,128]{3,2,1,0:T(8,128)S(1)} %fusion.14, bf16[4,64,64,128]{3,2,1,0:T(8,128)(2,1)S(1)} %copy-done.2, bf16[64,64]{1,0:T(8,128)(2,1)S(1)} %copy-done.5), kind=kOutput, calls=%fused_computation.11 | convolution fusion | flops 272629760 | bytes 16785408 | tf_op jit(solution)/shard_map/xyoz,co->xycz/dot_general | solution.py:167
  (80 shorter events, 14.5 us)
Async XLA Ops:
  0.6 48.6 %copy-start = (bf16[1,1,16,64,128]{4,3,2,1,0:T(8,128)(2,1)S(1)}, bf16[1,1,16,64,128]{4,3,2,1,0:T(8,128)(2,1)}, u32[]{:S(2)}) copy-start(bf16[1,1,16,64,128]{4,3,2,1,0:T(8,128)(2,1)} %param.6) | copy-start | bytes 786436
  7.5 3.4 %copy-start.3 = (f32[4,64,64,32]{2,1,0,3:T(8,128)S(1)}, f32[4,64,64,32]{2,1,0,3:T(8,128)}, u32[]{:S(2)}) copy-start(f32[4,64,64,32]{2,1,0,3:T(8,128)} %reshape.248) | copy-start | bytes 6291460
  35.2 13.8 %all-to-all-start.1 = ((bf16[16,2,1024]{2,1,0:T(2,128)(2,1)}), bf16[16,2,1024]{2,1,0:T(2,128)(2,1)S(1)}, u32[]{:S(2)}, u32[]{:S(2)}) async-start(bf16[16,2,1024]{2,1,0:T(2,128)(2,1)} %reshape.278), calls=%async_computation.1 | async-start | bytes 131072 | tf_op jit(solution)/shard_map/all_to_all | solution.py:143
  49.2 20.6 %copy-start.5 = (bf16[64,64]{1,0:T(8,128)(2,1)S(1)}, bf16[64,64]{1,0:T(8,128)(2,1)}, u32[]{:S(2)}) copy-start(bf16[64,64]{1,0:T(8,128)(2,1)} %param.7) | copy-start | bytes 24580
  50.6 11.1 %all-to-all-start.2 = ((bf16[16,2,1024]{2,1,0:T(2,128)(2,1)}), bf16[16,2,1024]{2,1,0:T(2,128)(2,1)S(1)}, u32[]{:S(2)}, u32[]{:S(2)}) async-start(bf16[16,2,1024]{2,1,0:T(2,128)(2,1)} %reshape.280), calls=%async_computation.2 | async-start | bytes 131072 | tf_op jit(solution)/shard_map/all_to_all | solution.py:147
  64.3 17.2 %all-to-all-start.3 = ((bf16[16,2,4096]{2,1,0:T(2,128)(2,1)}), bf16[16,2,4096]{2,1,0:T(2,128)(2,1)S(1)}, u32[]{:S(2)}, u32[]{:S(2)}) async-start(bf16[16,2,4096]{2,1,0:T(2,128)(2,1)} %reshape.282), calls=%async_computation.3 | async-start | bytes 524288 | tf_op jit(solution)/shard_map/all_to_all | solution.py:136
  81.9 2.2 %copy-start.6 = (bf16[1,4,64,64,128]{4,3,2,1,0:T(8,128)(2,1)S(1)}, bf16[1,4,64,64,128]{4,3,2,1,0:T(8,128)(2,1)}, u32[]{:S(2)}) copy-start(bf16[1,4,64,64,128]{4,3,2,1,0:T(8,128)(2,1)} %param.5) | copy-start | bytes 12582916
  82.8 4.0 %copy-start.4 = (f32[64,4,64,128]{3,0,2,1:T(8,128)S(1)}, f32[64,4,64,128]{3,0,2,1:T(8,128)}, u32[]{:S(2)}) copy-start(f32[64,4,64,128]{3,0,2,1:T(8,128)} %fusion.12) | copy-start | bytes 25165828
  92.3 4.1 %copy-start.1 = (bf16[4,64,64,128]{3,2,1,0:T(8,128)(2,1)}, bf16[4,64,64,128]{3,2,1,0:T(8,128)(2,1)S(1)}, u32[]{:S(2)}) copy-start(bf16[4,64,64,128]{3,2,1,0:T(8,128)(2,1)S(1)} %fusion.5) | copy-start | bytes 12582916
  101.5 14.4 %all-to-all-start.4 = ((bf16[16,2,4096]{2,1,0:T(2,128)(2,1)}), bf16[16,2,4096]{2,1,0:T(2,128)(2,1)S(1)}, u32[]{:S(2)}, u32[]{:S(2)}) async-start(bf16[16,2,4096]{2,1,0:T(2,128)(2,1)} %reshape.284), calls=%async_computation.4 | async-start | bytes 524288 | tf_op jit(solution)/shard_map/all_to_all | solution.py:127
  141.8 16.3 %all-to-all-start.7 = ((bf16[16,2,4096]{2,1,0:T(2,128)(2,1)}), bf16[16,2,4096]{2,1,0:T(2,128)(2,1)S(1)}, u32[]{:S(2)}, u32[]{:S(2)}) async-start(bf16[16,2,4096]{2,1,0:T(2,128)(2,1)} %reshape.290), calls=%async_computation.7 | async-start | bytes 524288 | tf_op jit(solution)/shard_map/all_to_all | solution.py:136
  160.6 2.2 %copy-start.2 = (bf16[4,64,64,128]{3,2,1,0:T(8,128)(2,1)S(1)}, bf16[4,64,64,128]{3,2,1,0:T(8,128)(2,1)}, u32[]{:S(2)}) copy-start(bf16[4,64,64,128]{3,2,1,0:T(8,128)(2,1)} %copy-done.1) | copy-start | bytes 12582916
where the time goes:
time: 168 us; the launch traced here: 166 us
  blocking collectives  40.7 us (24%)
  waiting for transfers between devices  39.4 us (23%)
  matrix products  38.7 us (23%)
  starting transfers between devices  25.1 us (15%)
  local copies, waits for them, and re-layouts  15.2 us (9%)
  other arithmetic  5.77 us (3%)
    all_to_all x1, blocking collectives, to_modes(): lax.all_to_all(sectioned.astype(jnp.bfloat16), 'pencil', split_axis=1, co...  20.2 us
    all_to_all x2, waiting for transfers between devices, to_grid(): lax.all_to_all(sectioned.astype(jnp.bfloat16), 'pencil', split_axis=0, co...  14.7 us
    unnamed x32, local copies, waits for them, and re-layouts  10.8 us
    all_to_all x2, starting transfers between devices, to_grid(): lax.all_to_all(sectioned.astype(jnp.bfloat16), 'pencil', split_axis=0, co...  10.7 us
    all_to_all x1, blocking collectives, to_owner(): lax.all_to_all(coeffs[None], 'dp', split_axis=1, concat_axis=0, tiled=True)  10.2 us
    all_to_all x1, blocking collectives, from_owner(): lax.all_to_all(coeffs.astype(jnp.bfloat16), 'dp', split_axis=0, concat_ax...  10.2 us
    all_to_all x1, waiting for transfers between devices, to_modes(): lax.all_to_all(sectioned.astype(jnp.bfloat16), 'pencil', split_axis=1, co...  9.59 us
    dot_general x2, matrix products, z_forward(): jnp.dot(field_in.reshape(-1, shape_in[-1]), matrix, preferred_element_typ...  7.76 us
  transfers between devices with their start and end apart: 5, of which 5 were waited for; matrix products, arithmetic and copies ran while one was open for 5% of the time, Pallas kernels for 0%

commit v1 on v0

v1 whole, which is shorter than its diff:
```python
import functools
import math

import jax
import jax.numpy as jnp
import numpy as np
from jax import lax
from jax.experimental import pallas as pl
from jax.experimental.pallas import tpu as pltpu
from jax.sharding import PartitionSpec as P

NX = 64
NY = 64
NZ = 128
CH = 64
MX = 16
MY = 16
MZ = 16
MESH = pl.DeviceIdType.MESH
F32 = jnp.float32
BF16 = jnp.bfloat16
CHUNKS = 2
HC = CH // CHUNKS
SCALE = 1.0 / (NX * NY * NZ)


def line_table():
    position = np.arange(NX)
    freq = np.arange(MX)
    freq = np.where(freq < MX // 2, freq, freq - MX)
    angle = 2.0 * math.pi * np.mod(position[:, None] * freq[None, :], NX) / NX
    cos, sin = np.cos(angle), np.sin(angle)
    table = np.zeros((16, 2, 4, MZ, 2, MX, MZ), np.float32)
    cosg, sing = cos.reshape(16, 4, MX), sin.reshape(16, 4, MX)
    for k in range(MZ):
        table[:, 0, :, k, 0, :, k] = cosg
        table[:, 1, :, k, 0, :, k] = sing
        table[:, 1, :, k, 1, :, k] = cosg
        table[:, 0, :, k, 1, :, k] = -sing
    return table.reshape(2048, 512)


def z_table():
    angle = 2.0 * math.pi * np.mod(np.arange(NZ)[:, None] * np.arange(MZ)[None, :], NZ) / NZ
    table = np.zeros((4, NZ, 2, 4, MZ), np.float32)
    for q in range(4):
        table[q, :, 0, q, :] = np.cos(angle)
        table[q, :, 1, q, :] = -np.sin(angle)
    return table.reshape(512, 128)


def dot(a, b):
    return jnp.dot(a, b, preferred_element_type=F32)


def dot_t(a, b):
    return lax.dot_general(a, b, (((1,), (1,)), ((), ())), preferred_element_type=F32)


def gelu_slope(pre):
    normal_cdf = 0.5 * (1.0 + lax.erf(pre * (1.0 / math.sqrt(2.0))))
    return normal_cdf + pre * jnp.exp(-0.5 * pre * pre) * (1.0 / math.sqrt(2.0 * math.pi))


def kernel(
    field_hbm, cot_hbm, w_hbm, wl_hbm, t_hbm, zf_hbm, out_hbm, gw_hbm,
    f_ref, c_ref, w_ref, wl_ref, t_ref, zf_ref, big, slope, out_v, gw_v,
    a2, ly, vy, xo, xi, wb, bw, xf, vf, ukeep,
    s0, r0, s1, r1, s2, r2, s3, r3,
    us, ur, vs, vr, gs, gr, ds_, dr,
    lsem, osem, ssem, rsem,
):
    me_d = lax.axis_index("dp")
    me_p = lax.axis_index("pencil")

    def load(src, dst, i):
        return pltpu.make_async_copy(src, dst, lsem.at[i])

    loads = [load(field_hbm.at[0, x], f_ref.at[x], x) for x in range(4)]
    loads += [
        load(zf_hbm, zf_ref, 4),
        load(t_hbm, t_ref, 5),
        load(w_hbm.at[0, 0], w_ref, 6),
        load(wl_hbm, wl_ref, 7),
        load(cot_hbm.at[0], c_ref, 8),
    ]
    for i in (4, 0, 1, 2, 3, 5, 6, 7, 8):
        loads[i].start()

    barrier = pltpu.get_barrier_semaphore()

    @pl.loop(1, 16)
    def _(d):
        pl.semaphore_signal(
            barrier, inc=1, device_id=(me_d, lax.rem(me_p + d, 16)), device_id_type=MESH
        )
        pl.semaphore_signal(
            barrier, inc=1, device_id=(lax.rem(me_d + d, 16), me_p), device_id_type=MESH
        )

    def send_pencil(e, sb, rb, h):
        rb[me_p, pl.ds(h * HC, HC)] = sb[me_p, pl.ds(h * HC, HC)]

        @pl.loop(1, 16)
        def _(d):
            to = lax.rem(me_p + d, 16)
            pltpu.make_async_remote_copy(
                src_ref=sb.at[to, pl.ds(h * HC, HC)],
                dst_ref=rb.at[me_p, pl.ds(h * HC, HC)],
                send_sem=ssem.at[e],
                recv_sem=rsem.at[e],
                device_id=(me_d, to),
                device_id_type=MESH,
            ).start()

    def send_dp(e, sb, rb):
        rb[me_d] = sb[me_d]

        @pl.loop(1, 16)
        def _(d):
            to = lax.rem(me_d + d, 16)
            pltpu.make_async_remote_copy(
                src_ref=sb.at[to],
                dst_ref=rb.at[me_d],
                send_sem=ssem.at[e],
                recv_sem=rsem.at[e],
                device_id=(to, me_p),
                device_id_type=MESH,
            ).start()

    def wait_pencil(sem, buf, h):
        part = buf.at[pl.ds(0, 15), pl.ds(h * HC, HC)]
        pltpu.make_async_copy(part, part, sem).wait()

    def wait_dp(sem, buf):
        part = buf.at[pl.ds(0, 15)]
        pltpu.make_async_copy(part, part, sem).wait()

    slot = lax.broadcasted_iota(jnp.int32, (HC, 128), 1) // 16
    masks = [slot == m for m in range(8)]

    def merge(pieces):
        out = pieces[0]
        for m in range(1, 8):
            out = jnp.where(masks[m], pieces[m], out)
        return out

    def roll(v, amount):
        amount %= 128
        return v if amount == 0 else pltpu.roll(v, amount, 1)

    def z_forward(x, h, get):
        lhs = jnp.concatenate([get(q).reshape(16 * HC, 128) for q in range(4)], axis=1)
        a = dot(lhs, zf_ref[...]).astype(BF16).reshape(16, HC, 128)
        row = pl.multiple_of(x * HC, HC)
        for g in range(16):
            a2[pl.ds(row, HC), g * 128 : (g + 1) * 128] = a[g]

    def y_forward(sb, h):
        y = dot(a2[...], t_ref[...])
        for jh in range(2):
            rolled = []
            for e in range(8):
                ri, x = e // 4, e % 4
                tile = y[x * HC : (x + 1) * HC, (ri * 2 + jh) * 128 : (ri * 2 + jh + 1) * 128]
                rolled.append(roll(tile, 16 * e))
            for j8 in range(8):
                res = merge([rolled[(m - j8) % 8] for m in range(8)])
                sb[jh * 8 + j8, h * HC : (h + 1) * HC, :] = roll(res, -16 * j8).astype(BF16)

    def y_inverse(rb, h):
        for jh in range(2):
            rolled = [
                roll(rb[jh * 8 + j8, h * HC : (h + 1) * HC, :].astype(F32), 16 * j8)
                for j8 in range(8)
            ]
            for e in range(8):
                ri, x = e // 4, e % 4
                res = merge([rolled[(m - e) % 8] for m in range(8)])
                ly[
                    x * HC : (x + 1) * HC, (ri * 2 + jh) * 128 : (ri * 2 + jh + 1) * 128
                ] = roll(res, -16 * e).astype(BF16)
        vy[...] = dot_t(ly[...], t_ref[...]).astype(BF16)

    def x_forward(rb, h):
        lhs = jnp.concatenate([rb[p, h * HC : (h + 1) * HC, :] for p in range(16)], axis=1)
        xo[h * HC : (h + 1) * HC, :] = dot(lhs, t_ref[...])

    def modes_out(dst, scale):
        both = jnp.concatenate([xo[:, :256], xo[:, 256:]], axis=0)
        turned = both.T.reshape(16, 16, 128)
        if scale is not None:
            turned = turned * scale
        dst[...] = turned.astype(BF16)

    def modes_in(src):
        both = src[...].astype(F32).reshape(256, 128).T
        xi[...] = jnp.concatenate([both[:64], both[64:]], axis=1).astype(BF16)

    def x_inverse(sb, h):
        o = dot_t(xi[h * HC : (h + 1) * HC, :], t_ref[...]).astype(BF16)
        for p in range(16):
            sb[p, h * HC : (h + 1) * HC, :] = o[:, p * 128 : (p + 1) * 128]

    def mix(lhs, src, dst):
        @pl.loop(0, 4)
        def _(x):
            @pl.loop(0, 8)
            def _(gp):
                g = gp * 2
                rhs = jnp.concatenate(
                    [src[x, g].reshape(256, 128), src[x, g + 1].reshape(256, 128)], axis=1
                )
                o = dot(lhs, rhs)
                dst[x, g] = o[:, :128].reshape(4, CH, 128)
                dst[x, g + 1] = o[:, 128:].reshape(4, CH, 128)

    load_z = loads[4]
    load_z.wait()
    for h in range(CHUNKS):
        for x in range(4):
            if h == 0:
                loads[x].wait()
            z_forward(x, h, lambda q: f_ref[x, :, q, h * HC : (h + 1) * HC, :])
        if h == 0:
            loads[5].wait()
        y_forward(s0, h)
        if h == 0:
            pl.semaphore_wait(barrier, 30)
        send_pencil(h, s0, r0, h)

    loads[6].wait()
    loads[7].wait()
    for k in range(MZ):
        w = w_ref[k].astype(F32)
        turned = pltpu.roll(w, 64, 1)
        lane = lax.broadcasted_iota(jnp.int32, (64, 128), 1)
        turned = jnp.where(lane < 64, -turned, turned)
        wb[k] = jnp.concatenate([w, turned], axis=0).astype(BF16)
    wl = wl_ref[...].astype(F32)
    wide = jnp.concatenate([wl] * 4, axis=1)
    tall = jnp.concatenate([wide] * 4, axis=0)
    row = lax.broadcasted_iota(jnp.int32, (256, 256), 0) // 64
    col = lax.broadcasted_iota(jnp.int32, (256, 256), 1) // 64
    block = jnp.where(row == col, tall, 0.0)
    bw[0] = block.T.astype(BF16)
    bw[1] = block.astype(BF16)
    mix(bw[0], f_ref, big)

    for h in range(CHUNKS):
        wait_pencil(rsem.at[h], r0, h)
        x_forward(r0, h)
    modes_out(us, None)
    send_dp(2, us, ur)
    wait_dp(rsem.at[2], ur)

    def regroup(src, keep):
        xf[...] = src[...].astype(F32).reshape(256, 128)
        for k in range(MZ):
            keep[k] = xf[pl.ds(k, 16, stride=16), :].astype(BF16)

    regroup(ur, ukeep.at[0])
    for k in range(MZ):
        scale = SCALE if k == 0 else 2.0 * SCALE
        vf[pl.ds(k, 16, stride=16), :] = dot(ukeep[0, k], wb[k]) * scale
    vs[...] = vf[...].astype(BF16).reshape(16, 16, 128)
    send_dp(3, vs, vr)
    wait_dp(rsem.at[3], vr)

    modes_in(vr)
    for h in range(CHUNKS):
        x_inverse(s1, h)
        send_pencil(4 + h, s1, r1, h)
    loads[8].wait()

    for h in range(CHUNKS):
        wait_pencil(rsem.at[4 + h], r1, h)
        y_inverse(r1, h)

        @pl.loop(0, 4)
        def _(x, h=h):
            row = pl.multiple_of(x * HC, HC)
            for gq in range(4):
                lhs = jnp.concatenate(
                    [vy[pl.ds(row, HC), g * 128 : (g + 1) * 128] for g in range(gq * 4, gq * 4 + 4)],
                    axis=0,
                )
                v = dot_t(lhs, zf_ref[...])
                parts = []
                for q in range(4):
                    pre = v[:, q * 128 : (q + 1) * 128].reshape(4, HC, 128)
                    at = (x, slice(gq * 4, gq * 4 + 4), q, slice(h * HC, (h + 1) * HC))
                    pre = pre + big[at]
                    sl = (c_ref[at].astype(F32) * gelu_slope(pre)).astype(BF16)
                    slope[at] = sl
                    parts.append(sl.reshape(4 * HC, 128))
                a = dot(jnp.concatenate(parts, axis=1), zf_ref[...]).astype(BF16)
                for i in range(4):
                    g = gq * 4 + i
                    a2[pl.ds(row, HC), g * 128 : (g + 1) * 128] = a[i * HC : (i + 1) * HC]

        y_forward(s2, h)
        send_pencil(6 + h, s2, r2, h)

    mix(bw[1], slope, big)

    for h in range(CHUNKS):
        wait_pencil(rsem.at[6 + h], r2, h)
        x_forward(r2, h)
    kk = lax.broadcasted_iota(jnp.int32, (16, 16, 128), 1)
    modes_out(gs, jnp.where(kk == 0, SCALE, 2.0 * SCALE).astype(F32))
    send_dp(8, gs, gr)
    wait_dp(rsem.at[8], gr)

    regroup(gr, ukeep.at[1])
    for k in range(MZ):
        vf[pl.ds(k, 16, stride=16), :] = dot_t(ukeep[1, k], wb[k])
    ds_[...] = vf[...].astype(BF16).reshape(16, 16, 128)
    send_dp(9, ds_, dr)

    lane = lax.broadcasted_iota(jnp.int32, (64, 128), 1)
    for k in range(MZ):
        cross = lax.dot_general(
            ukeep[0, k], ukeep[1, k], (((0,), (0,)), ((), ())), preferred_element_type=F32
        )
        low = pltpu.roll(cross[64:], 64, 1)
        gw_v[k] = cross[:64] + jnp.where(lane < 64, low, -low)
    gw_copy = pltpu.make_async_copy(gw_v, gw_hbm.at[0, 0], osem.at[2 * 4])
    gw_copy.start()

    wait_dp(rsem.at[9], dr)
    modes_in(dr)
    for h in range(CHUNKS):
        x_inverse(s3, h)
        send_pencil(10 + h, s3, r3, h)

    outs = []
    for h in range(CHUNKS):
        wait_pencil(rsem.at[10 + h], r3, h)
        y_inverse(r3, h)
        for x in range(4):
            for gq in range(4):
                lhs = jnp.concatenate(
                    [
                        vy[x * HC : (x + 1) * HC, g * 128 : (g + 1) * 128]
                        for g in range(gq * 4, gq * 4 + 4)
                    ],
                    axis=0,
                )
                v = dot_t(lhs, zf_ref[...])
                for q in range(4):
                    at = (x, slice(gq * 4, gq * 4 + 4), q, slice(h * HC, (h + 1) * HC))
                    out_v[at] = (v[:, q * 128 : (q + 1) * 128].reshape(4, HC, 128) + big[at]).astype(BF16)
            part = (x, slice(None), slice(None), pl.ds(h * HC, HC))
            copy = pltpu.make_async_copy(
                out_v.at[part], out_hbm.at[(0,) + part], osem.at[h * 4 + x]
            )
            copy.start()
            outs.append(copy)

    for h in range(CHUNKS):
        wait_pencil(ssem.at[h], s0, h)
        wait_pencil(ssem.at[4 + h], s1, h)
        wait_pencil(ssem.at[6 + h], s2, h)
        wait_pencil(ssem.at[10 + h], s3, h)
    wait_dp(ssem.at[2], us)
    wait_dp(ssem.at[3], vs)
    wait_dp(ssem.at[8], gs)
    wait_dp(ssem.at[9], ds_)
    gw_copy.wait()
    for copy in outs:
        copy.wait()


def body(field, cotangent, w_spec, w_local):
    table = jnp.asarray(line_table().astype(jnp.bfloat16))
    zf = jnp.asarray(z_table().astype(jnp.bfloat16))
    shape6 = (1, 4, 16, 4, CH, NZ)
    any_spec = pl.BlockSpec(memory_space=pl.ANY)
    pencil_buf = pltpu.VMEM((16, CH, 128), BF16)
    dp_buf = pltpu.VMEM((16, 16, 128), BF16)
    grid_f32 = pltpu.VMEM((4, 16, 4, CH, NZ), F32)
    grid_b16 = pltpu.VMEM((4, 16, 4, CH, NZ), BF16)
    out, gw = pl.pallas_call(
        kernel,
        out_shape=(
            jax.ShapeDtypeStruct(shape6, BF16),
            jax.ShapeDtypeStruct((1, 1, MZ, CH, 2 * CH), F32),
        ),
        in_specs=[any_spec] * 6,
        out_specs=[any_spec] * 2,
        scratch_shapes=[
            grid_b16,
            grid_b16,
            pltpu.VMEM((MZ, CH, 2 * CH), BF16),
            pltpu.VMEM((CH, CH), BF16),
            pltpu.VMEM((2048, 512), BF16),
            pltpu.VMEM((512, 128), BF16),
            grid_f32,
            grid_b16,
            grid_b16,
            pltpu.VMEM((MZ, CH, 2 * CH), F32),
            pltpu.VMEM((4 * HC, 2048), BF16),
            pltpu.VMEM((4 * HC, 512), BF16),
            pltpu.VMEM((4 * HC, 2048), BF16),
            pltpu.VMEM((CH, 512), F32),
            pltpu.VMEM((CH, 512), BF16),
            pltpu.VMEM((MZ, 128, 128), BF16),
            pltpu.VMEM((2, 256, 256), BF16),
            pltpu.VMEM((256, 128), F32),
            pltpu.VMEM((256, 128), F32),
            pltpu.VMEM((2, 16, 16, 128), BF16),
        ]
        + [pencil_buf] * 8
        + [dp_buf] * 8
        + [
            pltpu.SemaphoreType.DMA((9,)),
            pltpu.SemaphoreType.DMA((9,)),
            pltpu.SemaphoreType.DMA((12,)),
            pltpu.SemaphoreType.DMA((12,)),
        ],
        compiler_params=pltpu.CompilerParams(
            collective_id=0, has_side_effects=True, vmem_limit_bytes=60 * 1024 * 1024
        ),
        name="layer",
    )(field.reshape(shape6), cotangent.reshape(shape6), w_spec, w_local, table, zf)
    return (out.reshape(1, 4, NY, CH, NZ), gw)


def solution(mesh):
    placed = P("dp", "pencil", None, None, None)
    return jax.shard_map(
        body,
        mesh=mesh,
        in_specs=(placed, placed, placed, P()),
        out_specs=(placed, placed),
        check_vma=False,
    )
```

time: 168 us -> 88.3 us (0.53)
  Pallas kernels: 0 us -> 80.4 us
  blocking collectives: 40.7 us -> 0 us
  waiting for transfers between devices: 39.4 us -> 0 us
  matrix products: 38.7 us -> 0 us
  starting transfers between devices: 25.1 us -> 0 us
  local copies, waits for them, and re-layouts: 15.2 us -> 6.02 us
  other arithmetic: 5.77 us -> 0 us
    pallas_call x0 -> x1, Pallas kernels: none -> 80.4 us  [body(): pl.pallas_call(kernel, out_shape=(jax.ShapeDtypeStruct(shape6, BF16), jax...]
    all_to_all x3 -> x0, blocking collectives: 40.7 us -> none  [the longest x1 20.2 us: to_modes(): lax.all_to_all(sectioned.astype(jnp.bfloat16), 'pencil', split_axis=1, co...]
    all_to_all x5 -> x0, waiting for transfers between devices: 39.4 us -> none  [the longest x2 14.7 us: to_grid(): lax.all_to_all(sectioned.astype(jnp.bfloat16), 'pencil', split_axis=0, co...]
    dot_general x28 -> x0, matrix products: 38.7 us -> none  [the longest x2 7.76 us: z_forward(): jnp.dot(field_in.reshape(-1, shape_in[-1]), matrix, preferred_element_typ...]
    all_to_all x5 -> x0, starting transfers between devices: 25.1 us -> none  [the longest x2 10.7 us: to_grid(): lax.all_to_all(sectioned.astype(jnp.bfloat16), 'pencil', split_axis=0, co...]
    unnamed x32 -> x4, local copies, waits for them, and re-layouts: 10.8 us -> 6.02 us
    slice x7 -> x0, other arithmetic: 3.52 us -> none  [the longest x6 3.5 us: rotate_half(): return jnp.concatenate([values[..., middle:], -values[..., :middle]], -1)]
    reshape x1 -> x0, local copies, waits for them, and re-layouts: 3.02 us -> none  [z_forward(): return product.reshape(shape_in[:-1] + (matrix.shape[1],))]
  transfers between devices with their start and end apart: 5 -> 0, of which waited for: 5 -> 0; matrix products, arithmetic and copies ran while one was open for 5% -> 0% of each run, Pallas kernels for 0% -> 0%
where the time goes in v1:
time: 88.3 us; the launch traced here: 87.1 us
  Pallas kernels  80.4 us (91%)
  local copies, waits for them, and re-layouts  6.02 us (7%)
    pallas_call x1, Pallas kernels, body(): pl.pallas_call(kernel, out_shape=(jax.ShapeDtypeStruct(shape6, BF16), jax...  80.4 us
    unnamed x4, local copies, waits for them, and re-layouts  6.02 us

profile of v1, /device:TPU:8, one launch (start us, length us, event | category | flops | bytes accessed | tf_op | source)
XLA Modules:
  0.0 87.1 jit_solution(12909359068683770672)
XLA Ops:
  0.6 80.4 %layer.1 = (bf16[1,4,16,4,64,128]{5,4,3,2,1,0:T(8,128)(2,1)}, f32[1,1,16,64,128]{4,3,2,1,0:T(8,128)}) custom-call(bf16[1,4,16,4,64,128]{5,4,3,2,1,0:T(8,128)(2,1)} %bitcast.3, bf16[1,4,16,4,64,128]{5,4,3,2,1,0:T(8,128)(2,1)} %bitcast.4, bf16[1,1,16,64,128]{4,3,2,1,0:T(8,128)(2,1)} %w_hbm.1, bf16[64,64]{1,0:T(8,128)(2,1)} %wl_hbm.1, ...), custom_call_target="tpu_custom_call" | custom-call | tf_op jit(solution)/shard_map/layer/pallas_call | solution.py:384
  81.0 0.0 copy-start
  81.0 5.2 %copy.10 = bf16[1,4,64,64,128]{4,3,2,1,0:T(8,128)(2,1)} copy(bf16[1,4,64,64,128]{4,3,2,1,0:T(8,128)(2,1)} %bitcast.5) | data formatting | bytes 8388608
  86.3 0.0 copy-done
  86.3 0.8 copy.11
Async XLA Ops:
  81.0 5.2 %copy-start = (f32[1,1,16,64,128]{4,3,2,1,0:T(8,128)S(1)}, f32[1,1,16,64,128]{4,3,2,1,0:T(8,128)}, u32[]{:S(2)}) copy-start(f32[1,1,16,64,128]{4,3,2,1,0:T(8,128)} %get-tuple-element.9) | copy-start | bytes 1572868

commit v2 on v1

v2 whole, which is shorter than its diff:
```python
import functools
import math

import jax
import jax.numpy as jnp
import numpy as np
from jax import lax
from jax.experimental import pallas as pl
from jax.experimental.pallas import tpu as pltpu
from jax.sharding import PartitionSpec as P

NX = 64
NY = 64
NZ = 128
CH = 64
MX = 16
MY = 16
MZ = 16
KH = 8
MESH = pl.DeviceIdType.MESH
F32 = jnp.float32
BF16 = jnp.bfloat16
CHUNKS = 2
HC = CH // CHUNKS
SCALE = 1.0 / (NX * NY * NZ)


def line_table():
    position = np.arange(NX)
    freq = np.arange(MX)
    freq = np.where(freq < MX // 2, freq, freq - MX)
    angle = 2.0 * math.pi * np.mod(position[:, None] * freq[None, :], NX) / NX
    cos, sin = np.cos(angle).reshape(8, 2, 4, MX), np.sin(angle).reshape(8, 2, 4, MX)
    table = np.zeros((8, 2, 2, 4, KH, 2, MX, KH), np.float32)
    for k in range(KH):
        table[:, :, 0, :, k, 0, :, k] = cos
        table[:, :, 1, :, k, 0, :, k] = sin
        table[:, :, 1, :, k, 1, :, k] = cos
        table[:, :, 0, :, k, 1, :, k] = -sin
    return table.reshape(1024, 256)


def z_table():
    angle = 2.0 * math.pi * np.mod(np.arange(NZ)[:, None] * np.arange(MZ)[None, :], NZ) / NZ
    angle = angle.reshape(NZ, 2, KH)
    table = np.zeros((2, 4, NZ, 2, 2, 2, 4, KH), np.float32)
    for half in range(2):
        for q in range(4):
            table[half, q, :, :, half, 0, q, :] = np.cos(angle)
            table[half, q, :, :, half, 1, q, :] = -np.sin(angle)
    return table.reshape(1024, 256)


def dot(a, b):
    return jnp.dot(a, b, preferred_element_type=F32)


def dot_t(a, b):
    return lax.dot_general(a, b, (((1,), (1,)), ((), ())), preferred_element_type=F32)


def gelu_slope(pre):
    normal_cdf = 0.5 * (1.0 + lax.erf(pre * (1.0 / math.sqrt(2.0))))
    return normal_cdf + pre * jnp.exp(-0.5 * pre * pre) * (1.0 / math.sqrt(2.0 * math.pi))


def roll(v, amount):
    amount %= 128
    return v if amount == 0 else pltpu.roll(v, amount, 1)


def halves(low, high):
    lane = lax.broadcasted_iota(jnp.int32, low.shape, 1)
    return jnp.where(lane < 64, low, high)


def slot_masks(rows):
    slot = lax.broadcasted_iota(jnp.int32, (rows, 128), 1) // KH
    return [slot == m for m in range(16)]


def turn_slots(masks, get, put):
    rolled = [roll(get(j), KH * j) for j in range(16)]
    for e in range(16):
        out = rolled[(0 - e) % 16]
        for m in range(1, 16):
            out = jnp.where(masks[m], rolled[(m - e) % 16], out)
        put(e, roll(out, -KH * e))


def y_inverse(rb, c0, rows, ly):
    masks = slot_masks(rows)

    def put(e, tile):
        kh, ri, x = e // 8, (e // 4) % 2, e % 4
        at = (kh * 4 + x) * rows
        ly[at : at + rows, ri * 128 : (ri + 1) * 128] = tile.astype(BF16)

    turn_slots(masks, lambda j: rb[j, c0 : c0 + rows, :].astype(F32), put)


def kernel(
    field_hbm, cot_hbm, w_hbm, wl_hbm, t_hbm, tt_hbm, zf_hbm, zt_hbm,
    r3, sp_hbm, keep_hbm,
    f_ref, c_ref, w_ref, wl_ref, t_ref, tt_ref, zf_ref, zt_ref, big, slope, sp,
    a2, ly, vy, xo, xi, wb, bw, xf, vf, ukeep,
    s0, r0, s1, r1, s2, r2, s3,
    us, ur, vs, vr, gs, gr, ds_, dr,
    lsem, osem, ssem, rsem,
):
    me_d = lax.axis_index("dp")
    me_p = lax.axis_index("pencil")

    def load(src, dst, i):
        return pltpu.make_async_copy(src, dst, lsem.at[i])

    loads = [load(field_hbm.at[0, x], f_ref.at[x], x) for x in range(4)]
    loads += [
        load(zf_hbm, zf_ref, 4),
        load(t_hbm, t_ref, 5),
        load(w_hbm.at[0, 0], w_ref, 6),
        load(wl_hbm, wl_ref, 7),
        load(cot_hbm.at[0], c_ref, 8),
        load(tt_hbm, tt_ref, 9),
        load(zt_hbm, zt_ref, 10),
    ]
    for i in (4, 0, 1, 2, 3, 5, 6, 7, 9, 10, 8):
        loads[i].start()

    barrier = pltpu.get_barrier_semaphore()

    @pl.loop(1, 16)
    def _(d):
        pl.semaphore_signal(
            barrier, inc=1, device_id=(me_d, lax.rem(me_p + d, 16)), device_id_type=MESH
        )
        pl.semaphore_signal(
            barrier, inc=1, device_id=(lax.rem(me_d + d, 16), me_p), device_id_type=MESH
        )

    def send_pencil(e, sb, rb, h):
        @pl.loop(1, 16)
        def _(d):
            to = lax.rem(me_p + d, 16)
            pltpu.make_async_remote_copy(
                src_ref=sb.at[to, pl.ds(h * HC, HC)],
                dst_ref=rb.at[me_p, pl.ds(h * HC, HC)],
                send_sem=ssem.at[e],
                recv_sem=rsem.at[e],
                device_id=(me_d, to),
                device_id_type=MESH,
            ).start()

    def keep_pencil(sb, rb, h):
        rb[me_p, pl.ds(h * HC, HC)] = sb[me_p, pl.ds(h * HC, HC)]

    def send_dp(e, sb, rb):
        @pl.loop(1, 16)
        def _(d):
            to = lax.rem(me_d + d, 16)
            pltpu.make_async_remote_copy(
                src_ref=sb.at[to],
                dst_ref=rb.at[me_d],
                send_sem=ssem.at[e],
                recv_sem=rsem.at[e],
                device_id=(to, me_p),
                device_id_type=MESH,
            ).start()

        rb[me_d] = sb[me_d]

    def wait_pencil(sem, buf, h):
        part = buf.at[pl.ds(0, 15), pl.ds(h * HC, HC)]
        pltpu.make_async_copy(part, part, sem).wait()

    def wait_dp(sem, buf):
        part = buf.at[pl.ds(0, 15)]
        pltpu.make_async_copy(part, part, sem).wait()

    def z_store(a, x, g0, n):
        for i in range(n):
            for kh in range(2):
                row = pl.multiple_of((kh * 4 + x) * HC, HC)
                a2[pl.ds(row, HC), (g0 + i) * 128 : (g0 + i + 1) * 128] = a[
                    i * HC : (i + 1) * HC, kh * 128 : (kh + 1) * 128
                ]

    def y_forward(sb, h):
        y = dot(a2[...], t_ref[...])

        def get(e):
            kh, ri, x = e // 8, (e // 4) % 2, e % 4
            at = (kh * 4 + x) * HC
            return y[at : at + HC, ri * 128 : (ri + 1) * 128]

        def put(j, tile):
            sb[j, h * HC : (h + 1) * HC, :] = tile.astype(BF16)

        turn_slots(slot_masks(HC), get, put)

    def x_forward(rb, h):
        low, high = [], []
        for g in range(8):
            a = rb[2 * g, h * HC : (h + 1) * HC, :].astype(F32)
            b = roll(rb[2 * g + 1, h * HC : (h + 1) * HC, :].astype(F32), 64)
            low.append(halves(a, b).astype(BF16))
            high.append(roll(halves(b, a), 64).astype(BF16))
        lhs = jnp.concatenate(
            [jnp.concatenate(low, axis=1), jnp.concatenate(high, axis=1)], axis=0
        )
        o = dot(lhs, t_ref[...])
        for kh in range(2):
            xo[kh * CH + h * HC : kh * CH + (h + 1) * HC, :] = o[kh * HC : (kh + 1) * HC]

    def modes_out(dst, scaled):
        turned = xo[...].T
        if scaled:
            row = lax.broadcasted_iota(jnp.int32, (256, 128), 0)
            lane = lax.broadcasted_iota(jnp.int32, (256, 128), 1)
            zero = ((row % KH) == 0) & (lane < 64)
            turned = turned * jnp.where(zero, SCALE, 2.0 * SCALE)
        for j in range(16):
            dst[j] = jnp.concatenate(
                [turned[j * 8 : j * 8 + 8], turned[128 + j * 8 : 136 + j * 8]], axis=0
            ).astype(BF16)

    def modes_in(src):
        v = [src[j].astype(F32) for j in range(16)]
        both = jnp.concatenate([t[:8] for t in v] + [t[8:] for t in v], axis=0)
        xi[...] = both.T.astype(BF16)

    def x_inverse(sb, h):
        lhs = jnp.concatenate(
            [xi[kh * CH + h * HC : kh * CH + (h + 1) * HC, :] for kh in range(2)], axis=0
        )
        o = dot(lhs, tt_ref[...])
        for g in range(8):
            low = o[:HC, g * 128 : (g + 1) * 128]
            high = o[HC:, g * 128 : (g + 1) * 128]
            sb[2 * g, h * HC : (h + 1) * HC, :] = halves(low, roll(high, 64)).astype(BF16)
            sb[2 * g + 1, h * HC : (h + 1) * HC, :] = halves(roll(low, 64), high).astype(BF16)

    def mix(lhs, src, dst):
        @pl.loop(0, 4)
        def _(x):
            for g in range(8):
                rhs = jnp.concatenate(
                    [src[x, g, :4].reshape(256, 128), src[x, g, 4:].reshape(256, 128)], axis=1
                )
                o = dot(lhs, rhs).astype(dst.dtype)
                dst[x, g, :4] = o[:, :128].reshape(4, CH, 128)
                dst[x, g, 4:] = o[:, 128:].reshape(4, CH, 128)

    loads[4].wait()
    for h in range(CHUNKS):
        for x in range(4):
            if h == 0:
                loads[x].wait()
            lhs = jnp.concatenate(
                [
                    f_ref[x, :, p, h * HC : (h + 1) * HC, :].reshape(8 * HC, 128)
                    for p in range(8)
                ],
                axis=1,
            )
            z_store(dot(lhs, zf_ref[...]).astype(BF16), x, 0, 8)
        if h == 0:
            loads[5].wait()
        y_forward(s0, h)
        if h == 0:
            pl.semaphore_wait(barrier, 30)
        send_pencil(h, s0, r0, h)
        keep_pencil(s0, r0, h)

    loads[6].wait()
    loads[7].wait()
    lane64 = lax.broadcasted_iota(jnp.int32, (64, 128), 1)
    for k in range(MZ):
        w = w_ref[k].astype(F32)
        turned = roll(w, 64)
        turned = jnp.where(lane64 < 64, -turned, turned)
        wb[k] = jnp.concatenate([w, turned], axis=0).astype(BF16)
    wl = wl_ref[...].astype(F32)
    wide = jnp.concatenate([wl] * 4, axis=1)
    tall = jnp.concatenate([wide] * 4, axis=0)
    row = lax.broadcasted_iota(jnp.int32, (256, 256), 0) // 64
    col = lax.broadcasted_iota(jnp.int32, (256, 256), 1) // 64
    block = jnp.where(row == col, tall, 0.0)
    bw[0] = block.T.astype(BF16)
    bw[1] = block.astype(BF16)
    mix(bw[0], f_ref, big)

    for h in range(CHUNKS):
        wait_pencil(rsem.at[h], r0, h)
        x_forward(r0, h)
    modes_out(us, False)
    send_dp(2, us, ur)
    loads[9].wait()
    loads[10].wait()
    loads[8].wait()
    wait_dp(rsem.at[2], ur)

    def regroup(src, i):
        xf[...] = src[...].astype(F32).reshape(256, 128)
        for k in range(KH):
            re = xf[pl.ds(k, 16, stride=16), :]
            im = xf[pl.ds(KH + k, 16, stride=16), :]
            ukeep[i, k] = halves(re, roll(im, 64)).astype(BF16)
            ukeep[i, KH + k] = halves(roll(re, 64), im).astype(BF16)

    def products(mode, dst):
        for k in range(KH):
            low, high = mode(k), mode(KH + k)
            vf[pl.ds(k, 16, stride=16), :] = halves(low, roll(high, 64))
            vf[pl.ds(KH + k, 16, stride=16), :] = halves(roll(low, 64), high)
        dst[...] = vf[...].astype(BF16).reshape(16, 16, 128)

    regroup(ur, 0)
    products(lambda k: dot(ukeep[0, k], wb[k]) * (SCALE if k == 0 else 2.0 * SCALE), vs)
    send_dp(3, vs, vr)
    wait_dp(rsem.at[3], vr)

    modes_in(vr)
    for h in range(CHUNKS):
        x_inverse(s1, h)
        send_pencil(4 + h, s1, r1, h)
        keep_pencil(s1, r1, h)

    for h in range(CHUNKS):
        wait_pencil(rsem.at[4 + h], r1, h)
        y_inverse(r1, h * HC, HC, ly)
        vy[...] = dot(ly[...], tt_ref[...]).astype(BF16)

        @pl.loop(0, 4)
        def _(x, h=h):
            for g0 in (0, 4):
                parts = []
                for g in range(g0, g0 + 4):
                    rows = [pl.ds(pl.multiple_of((kh * 4 + x) * HC, HC), HC) for kh in range(2)]
                    parts.append(
                        jnp.concatenate([vy[r, g * 128 : (g + 1) * 128] for r in rows], axis=1)
                    )
                v = dot(jnp.concatenate(parts, axis=0), zt_ref[...])
                parts = []
                for p in range(8):
                    at = (x, slice(g0, g0 + 4), p, slice(h * HC, (h + 1) * HC))
                    pre = v[:, p * 128 : (p + 1) * 128].reshape(4, HC, 128) + big[at]
                    sl = (c_ref[at].astype(F32) * gelu_slope(pre)).astype(BF16)
                    slope[at] = sl
                    parts.append(sl.reshape(4 * HC, 128))
                z_store(dot(jnp.concatenate(parts, axis=1), zf_ref[...]).astype(BF16), x, g0, 4)

        y_forward(s2, h)
        send_pencil(6 + h, s2, r2, h)
        keep_pencil(s2, r2, h)

    mix(bw[1], slope, sp)
    sp_copy = pltpu.make_async_copy(sp, sp_hbm, osem.at[0])
    sp_copy.start()

    for h in range(CHUNKS):
        wait_pencil(rsem.at[6 + h], r2, h)
        x_forward(r2, h)
    modes_out(gs, True)
    send_dp(8, gs, gr)
    wait_dp(rsem.at[8], gr)

    regroup(gr, 1)
    products(lambda k: dot_t(ukeep[1, k], wb[k]), ds_)
    send_dp(9, ds_, dr)
    keep_copy = pltpu.make_async_copy(ukeep, keep_hbm, osem.at[1])
    keep_copy.start()
    wait_dp(rsem.at[9], dr)

    modes_in(dr)
    own = []
    for h in range(CHUNKS):
        x_inverse(s3, h)
        send_pencil(10 + h, s3, r3, h)
        part = pl.ds(h * HC, HC)
        own.append(pltpu.make_async_copy(s3.at[me_p, part], r3.at[me_p, part], osem.at[2 + h]))
        own[h].start()

    for h in range(CHUNKS):
        wait_pencil(ssem.at[h], s0, h)
        wait_pencil(ssem.at[4 + h], s1, h)
        wait_pencil(ssem.at[6 + h], s2, h)
    wait_dp(ssem.at[2], us)
    wait_dp(ssem.at[3], vs)
    wait_dp(ssem.at[8], gs)
    wait_dp(ssem.at[9], ds_)
    sp_copy.wait()
    keep_copy.wait()
    for h in range(CHUNKS):
        own[h].wait()
        wait_pencil(ssem.at[10 + h], s3, h)
        wait_pencil(rsem.at[10 + h], r3, h)


def last_kernel(
    r_hbm, sp_hbm, keep_hbm, tt_hbm, zt_hbm, out_hbm, gw_hbm,
    r_ref, sp, keep, tt_ref, zt_ref, ly, vy, out_v, gw_v, lsem, osem,
):
    loads = [
        pltpu.make_async_copy(r_hbm, r_ref, lsem.at[0]),
        pltpu.make_async_copy(tt_hbm, tt_ref, lsem.at[1]),
        pltpu.make_async_copy(zt_hbm, zt_ref, lsem.at[2]),
        pltpu.make_async_copy(keep_hbm, keep, lsem.at[3]),
    ]
    loads += [pltpu.make_async_copy(sp_hbm.at[x], sp.at[x], lsem.at[4 + x]) for x in range(4)]
    for copy in loads:
        copy.start()
    loads[0].wait()
    y_inverse(r_ref, 0, CH, ly)
    loads[1].wait()
    vy[...] = dot(ly[...], tt_ref[...]).astype(BF16)
    loads[2].wait()
    outs = []
    for x in range(4):
        loads[4 + x].wait()
        for g in range(8):
            lhs = jnp.concatenate(
                [
                    vy[(kh * 4 + x) * CH : (kh * 4 + x + 1) * CH, g * 128 : (g + 1) * 128]
                    for kh in range(2)
                ],
                axis=1,
            )
            v = dot(lhs, zt_ref[...])
            for p in range(8):
                out_v[x, g, p] = (v[:, p * 128 : (p + 1) * 128] + sp[x, g, p].astype(F32)).astype(BF16)
        outs.append(pltpu.make_async_copy(out_v.at[x], out_hbm.at[0, x], osem.at[x]))
        outs[x].start()

    loads[3].wait()
    lane = lax.broadcasted_iota(jnp.int32, (64, 128), 1)
    for k in range(MZ):
        cross = lax.dot_general(
            keep[0, k], keep[1, k], (((0,), (0,)), ((), ())), preferred_element_type=F32
        )
        low = roll(cross[64:], 64)
        gw_v[k] = cross[:64] + jnp.where(lane < 64, low, -low)
    outs.append(pltpu.make_async_copy(gw_v, gw_hbm.at[0, 0], osem.at[4]))
    outs[4].start()
    for copy in outs:
        copy.wait()


def body(field, cotangent, w_spec, w_local):
    table, zf = line_table(), z_table()
    t, tt, zf, zt = (jnp.asarray(m.astype(jnp.bfloat16)) for m in (table, table.T, zf, zf.T))
    grid = (4, 8, 8, CH, NZ)
    any_spec = pl.BlockSpec(memory_space=pl.ANY)
    pencil_buf = pltpu.VMEM((16, CH, 128), BF16)
    dp_buf = pltpu.VMEM((16, 16, 128), BF16)
    grid_b16 = pltpu.VMEM(grid, BF16)
    line = pltpu.VMEM((1024, 256), BF16)
    line_t = pltpu.VMEM((256, 1024), BF16)
    keep = pltpu.VMEM((2, MZ, 16, 128), BF16)
    r3, sp, kept = pl.pallas_call(
        kernel,
        out_shape=(
            jax.ShapeDtypeStruct((16, CH, 128), BF16),
            jax.ShapeDtypeStruct(grid, BF16),
            jax.ShapeDtypeStruct((2, MZ, 16, 128), BF16),
        ),
        in_specs=[any_spec] * 8,
        out_specs=[any_spec] * 3,
        scratch_shapes=[
            grid_b16,
            grid_b16,
            pltpu.VMEM((MZ, CH, 2 * CH), BF16),
            pltpu.VMEM((CH, CH), BF16),
            line,
            line_t,
            line,
            line_t,
            pltpu.VMEM(grid, F32),
            grid_b16,
            grid_b16,
            pltpu.VMEM((8 * HC, 1024), BF16),
            pltpu.VMEM((8 * HC, 256), BF16),
            pltpu.VMEM((8 * HC, 1024), BF16),
            pltpu.VMEM((128, 256), F32),
            pltpu.VMEM((128, 256), BF16),
            pltpu.VMEM((MZ, 128, 128), BF16),
            pltpu.VMEM((2, 256, 256), BF16),
            pltpu.VMEM((256, 128), F32),
            pltpu.VMEM((256, 128), F32),
            keep,
        ]
        + [pencil_buf] * 7
        + [dp_buf] * 8
        + [
            pltpu.SemaphoreType.DMA((11,)),
            pltpu.SemaphoreType.DMA((4,)),
            pltpu.SemaphoreType.DMA((12,)),
            pltpu.SemaphoreType.DMA((12,)),
        ],
        compiler_params=pltpu.CompilerParams(
            collective_id=0, has_side_effects=True, vmem_limit_bytes=60 * 1024 * 1024
        ),
        name="layer",
    )(field.reshape((1,) + grid), cotangent.reshape((1,) + grid), w_spec, w_local, t, tt, zf, zt)
    out, gw = pl.pallas_call(
        last_kernel,
        out_shape=(
            jax.ShapeDtypeStruct((1,) + grid, BF16),
            jax.ShapeDtypeStruct((1, 1, MZ, CH, 2 * CH), F32),
        ),
        in_specs=[any_spec] * 5,
        out_specs=[any_spec] * 2,
        scratch_shapes=[
            pencil_buf,
            grid_b16,
            keep,
            line_t,
            line_t,
            pltpu.VMEM((8 * CH, 256), BF16),
            pltpu.VMEM((8 * CH, 1024), BF16),
            grid_b16,
            pltpu.VMEM((MZ, CH, 2 * CH), F32),
            pltpu.SemaphoreType.DMA((8,)),
            pltpu.SemaphoreType.DMA((5,)),
        ],
        compiler_params=pltpu.CompilerParams(vmem_limit_bytes=60 * 1024 * 1024),
        name="last",
    )(r3, sp, kept, tt, zt)
    return (out.reshape(1, 4, NY, CH, NZ), gw)


def solution(mesh):
    placed = P("dp", "pencil", None, None, None)
    return jax.shard_map(
        body,
        mesh=mesh,
        in_specs=(placed, placed, placed, P()),
        out_specs=(placed, placed),
        check_vma=False,
    )
```

time: 88.3 us -> 81 us (0.917)
  local copies, waits for them, and re-layouts: 6.02 us -> 0 us
  Pallas kernels: 80.4 us -> 79.3 us
    unnamed x4 -> x0, local copies, waits for them, and re-layouts: 6.02 us -> none
    pallas_call x1 -> x2, Pallas kernels: 80.4 us -> 79.3 us  [the longest x1 72.6 us: body(): pl.pallas_call(kernel, out_shape=(jax.ShapeDtypeStruct((16, CH, 128), BF1...]
where the time goes in v2:
time: 81 us; the launch traced here: 80.1 us
  Pallas kernels  79.3 us (98%)
    pallas_call x1, Pallas kernels, body(): pl.pallas_call(kernel, out_shape=(jax.ShapeDtypeStruct((16, CH, 128), BF1...  72.6 us
    pallas_call x1, Pallas kernels, body(): pl.pallas_call(last_kernel, out_shape=(jax.ShapeDtypeStruct((1,) + grid,...  6.62 us

profile of v2, /device:TPU:8, one launch (start us, length us, event | category | flops | bytes accessed | tf_op | source)
XLA Modules:
  0.0 80.1 jit_solution(7190024682583556898)
XLA Ops:
  0.6 72.6 %layer.1 = (bf16[16,64,128]{2,1,0:T(8,128)(2,1)}, bf16[4,8,8,64,128]{4,3,2,1,0:T(8,128)(2,1)}, bf16[2,16,16,128]{3,2,1,0:T(8,128)(2,1)}) custom-call(bf16[1,4,8,8,64,128]{5,4,3,2,1,0:T(8,128)(2,1)} %bitcast.3, bf16[1,4,8,8,64,128]{5,4,3,2,1,0:T(8,128)(2,1)} %bitcast.4, bf16[1,1,16,64,128]{4,3,2,1,0:T(8,128)(2,1)} %w_hbm.1, bf16[64,64]{1,0:T(8,128)(2,1)} %wl_hbm.1, ...), custom_call_target="tpu_custom_call" | custom-call | tf_op jit(solution)/shard_map/layer/pallas_call | solution.py:460
  73.3 6.6 %last.1 = (bf16[1,4,8,8,64,128]{5,4,3,2,1,0:T(8,128)(2,1)}, f32[1,1,16,64,128]{4,3,2,1,0:T(8,128)}) custom-call(bf16[16,64,128]{2,1,0:T(8,128)(2,1)} %get-tuple-element.7.r_hbm, bf16[4,8,8,64,128]{4,3,2,1,0:T(8,128)(2,1)} %get-tuple-element.8.sp_hbm, bf16[2,16,16,128]{3,2,1,0:T(8,128)(2,1)} %get-tuple-element.9.keep_hbm, ...), custom_call_target="tpu_custom_call" | custom-call | tf_op jit(solution)/shard_map/last/pallas_call | solution.py:505

commit v3 on v2

--- a/solution.py
+++ b/solution.py
@@ -59,9 +59,9 @@
     return lax.dot_general(a, b, (((1,), (1,)), ((), ())), preferred_element_type=F32)
 
 
-def gelu_slope(pre):
-    normal_cdf = 0.5 * (1.0 + lax.erf(pre * (1.0 / math.sqrt(2.0))))
-    return normal_cdf + pre * jnp.exp(-0.5 * pre * pre) * (1.0 / math.sqrt(2.0 * math.pi))
+def gelu_slope(t):
+    bell = jnp.exp2(t * t * (-1.0 / math.log(2.0)) - 0.5 * math.log2(math.pi))
+    return 0.5 * lax.erf(t) + (t * bell + 0.5)
 
 
 def roll(v, amount):
@@ -101,8 +101,8 @@
 
 def kernel(
     field_hbm, cot_hbm, w_hbm, wl_hbm, t_hbm, tt_hbm, zf_hbm, zt_hbm,
-    r3, sp_hbm, keep_hbm,
-    f_ref, c_ref, w_ref, wl_ref, t_ref, tt_ref, zf_ref, zt_ref, big, slope, sp,
+    r3, sp_hbm, gw_hbm,
+    f_ref, c_ref, w_ref, wl_ref, t_ref, tt_ref, zf_ref, zt_ref, big, slope, sp, gw_v,
     a2, ly, vy, xo, xi, wb, bw, xf, vf, ukeep,
     s0, r0, s1, r1, s2, r2, s3,
     us, ur, vs, vr, gs, gr, ds_, dr,
@@ -240,14 +240,15 @@
             sb[2 * g, h * HC : (h + 1) * HC, :] = halves(low, roll(high, 64)).astype(BF16)
             sb[2 * g + 1, h * HC : (h + 1) * HC, :] = halves(roll(low, 64), high).astype(BF16)
 
-    def mix(lhs, src, dst):
+    def mix(lhs, src, dst, scale):
         @pl.loop(0, 4)
         def _(x):
             for g in range(8):
                 rhs = jnp.concatenate(
                     [src[x, g, :4].reshape(256, 128), src[x, g, 4:].reshape(256, 128)], axis=1
                 )
-                o = dot(lhs, rhs).astype(dst.dtype)
+                o = dot(lhs, rhs)
+                o = (o if scale is None else o * scale).astype(dst.dtype)
                 dst[x, g, :4] = o[:, :128].reshape(4, CH, 128)
                 dst[x, g, 4:] = o[:, 128:].reshape(4, CH, 128)
 
@@ -288,7 +289,7 @@
     block = jnp.where(row == col, tall, 0.0)
     bw[0] = block.T.astype(BF16)
     bw[1] = block.astype(BF16)
-    mix(bw[0], f_ref, big)
+    mix(bw[0], f_ref, big, math.sqrt(0.5))
 
     for h in range(CHUNKS):
         wait_pencil(rsem.at[h], r0, h)
@@ -316,7 +317,8 @@
         dst[...] = vf[...].astype(BF16).reshape(16, 16, 128)
 
     regroup(ur, 0)
-    products(lambda k: dot(ukeep[0, k], wb[k]) * (SCALE if k == 0 else 2.0 * SCALE), vs)
+    root = math.sqrt(0.5)
+    products(lambda k: dot(ukeep[0, k], wb[k]) * (root * SCALE if k == 0 else 2.0 * root * SCALE), vs)
     send_dp(3, vs, vr)
     wait_dp(rsem.at[3], vr)
 
@@ -331,30 +333,34 @@
         y_inverse(r1, h * HC, HC, ly)
         vy[...] = dot(ly[...], tt_ref[...]).astype(BF16)
 
-        @pl.loop(0, 4)
-        def _(x, h=h):
-            for g0 in (0, 4):
+        @pl.loop(0, 2)
+        def _(x2, h=h):
+            for xi_ in range(2):
+                x = 2 * x2 + xi_
+                rows = [pl.ds(pl.multiple_of((kh * 4 + x) * HC, HC), HC) for kh in range(2)]
+                lhs = jnp.concatenate(
+                    [
+                        jnp.concatenate([vy[r, g * 128 : (g + 1) * 128] for r in rows], axis=1)
+                        for g in range(8)
+                    ],
+                    axis=0,
+                )
                 parts = []
-                for g in range(g0, g0 + 4):
-                    rows = [pl.ds(pl.multiple_of((kh * 4 + x) * HC, HC), HC) for kh in range(2)]
-                    parts.append(
-                        jnp.concatenate([vy[r, g * 128 : (g + 1) * 128] for r in rows], axis=1)
-                    )
-                v = dot(jnp.concatenate(parts, axis=0), zt_ref[...])
-                parts = []
-                for p in range(8):
-                    at = (x, slice(g0, g0 + 4), p, slice(h * HC, (h + 1) * HC))
-                    pre = v[:, p * 128 : (p + 1) * 128].reshape(4, HC, 128) + big[at]
-                    sl = (c_ref[at].astype(F32) * gelu_slope(pre)).astype(BF16)
-                    slope[at] = sl
-                    parts.append(sl.reshape(4 * HC, 128))
-                z_store(dot(jnp.concatenate(parts, axis=1), zf_ref[...]).astype(BF16), x, g0, 4)
+                for n in range(4):
+                    v = dot(lhs, zt_ref[:, n * 256 : (n + 1) * 256])
+                    for i in range(2):
+                        at = (x, slice(None), 2 * n + i, slice(h * HC, (h + 1) * HC))
+                        pre = v[:, i * 128 : (i + 1) * 128].reshape(8, HC, 128) + big[at]
+                        sl = (c_ref[at].astype(F32) * gelu_slope(pre)).astype(BF16)
+                        slope[at] = sl
+                        parts.append(sl.reshape(8 * HC, 128))
+                z_store(dot(jnp.concatenate(parts, axis=1), zf_ref[...]).astype(BF16), x, 0, 8)
 
         y_forward(s2, h)
         send_pencil(6 + h, s2, r2, h)
         keep_pencil(s2, r2, h)
 
-    mix(bw[1], slope, sp)
+    mix(bw[1], slope, sp, None)
     sp_copy = pltpu.make_async_copy(sp, sp_hbm, osem.at[0])
     sp_copy.start()
 
@@ -368,8 +374,6 @@
     regroup(gr, 1)
     products(lambda k: dot_t(ukeep[1, k], wb[k]), ds_)
     send_dp(9, ds_, dr)
-    keep_copy = pltpu.make_async_copy(ukeep, keep_hbm, osem.at[1])
-    keep_copy.start()
     wait_dp(rsem.at[9], dr)
 
     modes_in(dr)
@@ -380,6 +384,15 @@
         part = pl.ds(h * HC, HC)
         own.append(pltpu.make_async_copy(s3.at[me_p, part], r3.at[me_p, part], osem.at[2 + h]))
         own[h].start()
+
+    for k in range(MZ):
+        cross = lax.dot_general(
+            ukeep[0, k], ukeep[1, k], (((0,), (0,)), ((), ())), preferred_element_type=F32
+        )
+        low = roll(cross[64:], 64)
+        gw_v[k] = cross[:64] + jnp.where(lane64 < 64, low, -low)
+    gw_copy = pltpu.make_async_copy(gw_v, gw_hbm, osem.at[1])
+    gw_copy.start()
 
     for h in range(CHUNKS):
         wait_pencil(ssem.at[h], s0, h)
@@ -390,7 +403,7 @@
     wait_dp(ssem.at[8], gs)
     wait_dp(ssem.at[9], ds_)
     sp_copy.wait()
-    keep_copy.wait()
+    gw_copy.wait()
     for h in range(CHUNKS):
         own[h].wait()
         wait_pencil(ssem.at[10 + h], s3, h)
@@ -398,14 +411,14 @@
 
 
 def last_kernel(
-    r_hbm, sp_hbm, keep_hbm, tt_hbm, zt_hbm, out_hbm, gw_hbm,
-    r_ref, sp, keep, tt_ref, zt_ref, ly, vy, out_v, gw_v, lsem, osem,
+    r_hbm, sp_hbm, gw_in, tt_hbm, zt_hbm, out_hbm, gw_hbm,
+    r_ref, sp, tt_ref, zt_ref, ly, vy, out_v, gw_v, lsem, osem,
 ):
     loads = [
         pltpu.make_async_copy(r_hbm, r_ref, lsem.at[0]),
         pltpu.make_async_copy(tt_hbm, tt_ref, lsem.at[1]),
         pltpu.make_async_copy(zt_hbm, zt_ref, lsem.at[2]),
-        pltpu.make_async_copy(keep_hbm, keep, lsem.at[3]),
+        pltpu.make_async_copy(gw_in, gw_v, lsem.at[3]),
     ]
     loads += [pltpu.make_async_copy(sp_hbm.at[x], sp.at[x], lsem.at[4 + x]) for x in range(4)]
     for copy in loads:
@@ -418,32 +431,33 @@
     outs = []
     for x in range(4):
         loads[4 + x].wait()
-        for g in range(8):
-            lhs = jnp.concatenate(
-                [
-                    vy[(kh * 4 + x) * CH : (kh * 4 + x + 1) * CH, g * 128 : (g + 1) * 128]
-                    for kh in range(2)
-                ],
-                axis=1,
-            )
-            v = dot(lhs, zt_ref[...])
-            for p in range(8):
-                out_v[x, g, p] = (v[:, p * 128 : (p + 1) * 128] + sp[x, g, p].astype(F32)).astype(BF16)
+        lhs = jnp.concatenate(
+            [
+                jnp.concatenate(
+                    [
+                        vy[(kh * 4 + x) * CH : (kh * 4 + x + 1) * CH, g * 128 : (g + 1) * 128]
+                        for kh in range(2)
+                    ],
+                    axis=1,
+                )
+                for g in range(8)
+            ],
+            axis=0,
+        )
+        for n in range(4):
+            v = dot(lhs, zt_ref[:, n * 256 : (n + 1) * 256])
+            for i in range(2):
+                part = v[:, i * 128 : (i + 1) * 128].reshape(8, CH, 128)
+                out_v[x, :, 2 * n + i] = (part + sp[x, :, 2 * n + i].astype(F32)).astype(BF16)
         outs.append(pltpu.make_async_copy(out_v.at[x], out_hbm.at[0, x], osem.at[x]))
         outs[x].start()
-
-    loads[3].wait()
-    lane = lax.broadcasted_iota(jnp.int32, (64, 128), 1)
-    for k in range(MZ):
-        cross = lax.dot_general(
-            keep[0, k], keep[1, k], (((0,), (0,)), ((), ())), preferred_element_type=F32
-        )
-        low = roll(cross[64:], 64)
-        gw_v[k] = cross[:64] + jnp.where(lane < 64, low, -low)
-    outs.append(pltpu.make_async_copy(gw_v, gw_hbm.at[0, 0], osem.at[4]))
-    outs[4].start()
+        if x == 0:
+            loads[3].wait()
+            outs_gw = pltpu.make_async_copy(gw_v, gw_hbm.at[0, 0], osem.at[4])
+            outs_gw.start()
     for copy in outs:
         copy.wait()
+    outs_gw.wait()
 
 
 def body(field, cotangent, w_spec, w_local):
@@ -457,12 +471,12 @@
     line = pltpu.VMEM((1024, 256), BF16)
     line_t = pltpu.VMEM((256, 1024), BF16)
     keep = pltpu.VMEM((2, MZ, 16, 128), BF16)
-    r3, sp, kept = pl.pallas_call(
+    r3, sp, gw = pl.pallas_call(
         kernel,
         out_shape=(
             jax.ShapeDtypeStruct((16, CH, 128), BF16),
             jax.ShapeDtypeStruct(grid, BF16),
-            jax.ShapeDtypeStruct((2, MZ, 16, 128), BF16),
+            jax.ShapeDtypeStruct((MZ, CH, 2 * CH), F32),
         ),
         in_specs=[any_spec] * 8,
         out_specs=[any_spec] * 3,
@@ -478,6 +492,7 @@
             pltpu.VMEM(grid, F32),
             grid_b16,
             grid_b16,
+            pltpu.VMEM((MZ, CH, 2 * CH), F32),
             pltpu.VMEM((8 * HC, 1024), BF16),
             pltpu.VMEM((8 * HC, 256), BF16),
             pltpu.VMEM((8 * HC, 1024), BF16),
@@ -513,7 +528,6 @@
         scratch_shapes=[
             pencil_buf,
             grid_b16,
-            keep,
             line_t,
             line_t,
             pltpu.VMEM((8 * CH, 256), BF16),
@@ -525,7 +539,7 @@
         ],
         compiler_params=pltpu.CompilerParams(vmem_limit_bytes=60 * 1024 * 1024),
         name="last",
-    )(r3, sp, kept, tt, zt)
+    )(r3, sp, gw, tt, zt)
     return (out.reshape(1, 4, NY, CH, NZ), gw)
 
 

time: 81 us -> 77.5 us (0.957)
  Pallas kernels: 79.3 us -> 76 us
    pallas_call x1, Pallas kernels: 6.62 us -> 4.74 us  [body(): pl.pallas_call(last_kernel, out_shape=(jax.ShapeDtypeStruct((1,) + grid,...]
    pallas_call x1, Pallas kernels: 72.6 us -> 71.3 us  [body(): pl.pallas_call(kernel, out_shape=(jax.ShapeDtypeStruct((16, CH, 128), BF1...]
where the time goes in v3:
time: 77.5 us; the launch traced here: 76.8 us
  Pallas kernels  76 us (98%)
  between operations  0.8 us (1%)
    pallas_call x1, Pallas kernels, body(): pl.pallas_call(kernel, out_shape=(jax.ShapeDtypeStruct((16, CH, 128), BF1...  71.3 us
    pallas_call x1, Pallas kernels, body(): pl.pallas_call(last_kernel, out_shape=(jax.ShapeDtypeStruct((1,) + grid,...  4.74 us

profile of v3, /device:TPU:8, one launch (start us, length us, event | category | flops | bytes accessed | tf_op | source)
XLA Modules:
  0.0 76.8 jit_solution(2809397733476726016)
XLA Ops:
  0.6 71.3 %layer.1 = (bf16[16,64,128]{2,1,0:T(8,128)(2,1)}, bf16[4,8,8,64,128]{4,3,2,1,0:T(8,128)(2,1)}, f32[16,64,128]{2,1,0:T(8,128)}) custom-call(bf16[1,4,8,8,64,128]{5,4,3,2,1,0:T(8,128)(2,1)} %bitcast.3, bf16[1,4,8,8,64,128]{5,4,3,2,1,0:T(8,128)(2,1)} %bitcast.4, bf16[1,1,16,64,128]{4,3,2,1,0:T(8,128)(2,1)} %w_hbm.1, bf16[64,64]{1,0:T(8,128)(2,1)} %wl_hbm.1, ...), custom_call_target="tpu_custom_call" | custom-call | tf_op jit(solution)/shard_map/layer/pallas_call | solution.py:474
  71.9 4.7 %last.1 = (bf16[1,4,8,8,64,128]{5,4,3,2,1,0:T(8,128)(2,1)}, f32[1,1,16,64,128]{4,3,2,1,0:T(8,128)}) custom-call(bf16[16,64,128]{2,1,0:T(8,128)(2,1)} %get-tuple-element.7.r_hbm, bf16[4,8,8,64,128]{4,3,2,1,0:T(8,128)(2,1)} %get-tuple-element.8.sp_hbm, f32[16,64,128]{2,1,0:T(8,128)} %get-tuple-element.9.gw_in, bf16[256,1024]{1,0:T(8,128)(2,1)} %constant.9.clone.tt_hbm, ...), custom_call_target="tpu_custom_call" | custom-call | tf_op jit(solution)/shard_map/last/pallas_call | solution.py:520

commit v4 on v3

--- a/solution.py
+++ b/solution.py
@@ -102,14 +102,17 @@
 def kernel(
     field_hbm, cot_hbm, w_hbm, wl_hbm, t_hbm, tt_hbm, zf_hbm, zt_hbm,
     r3, sp_hbm, gw_hbm,
-    f_ref, c_ref, w_ref, wl_ref, t_ref, tt_ref, zf_ref, zt_ref, big, slope, sp, gw_v,
-    a2, ly, vy, xo, xi, wb, bw, xf, vf, ukeep,
+    f_ref, c_ref, wall, wl_ref, t_ref, tt_ref, zf_ref, zt_ref, big, slope, sp, gw_v,
+    a2, ly, vy, xo, xi, bw, xf, ukeep,
     s0, r0, s1, r1, s2, r2, s3,
-    us, ur, vs, vr, gs, gr, ds_, dr,
-    lsem, osem, ssem, rsem,
+    us, ur, gs, gr, row_u, row_v, back_v, row_g, row_d, back_d,
+    lsem, osem, ssem, rsem, wssem, wrsem, yssem, yrsem,
 ):
     me_d = lax.axis_index("dp")
     me_p = lax.axis_index("pencil")
+    me_x, me_y, me_c = me_d // 4, lax.rem(me_d // 2, 2), lax.rem(me_d, 2)
+    x_up, x_down, x_far = lax.rem(me_x + 1, 4), lax.rem(me_x + 3, 4), lax.rem(me_x + 2, 4)
+    partner = me_d + 2 - 4 * me_y
 
     def load(src, dst, i):
         return pltpu.make_async_copy(src, dst, lsem.at[i])
@@ -118,7 +121,7 @@
     loads += [
         load(zf_hbm, zf_ref, 4),
         load(t_hbm, t_ref, 5),
-        load(w_hbm.at[0, 0], w_ref, 6),
+        load(w_hbm.at[0, 0], wall.at[2 * me_x + me_c], 6),
         load(wl_hbm, wl_ref, 7),
         load(cot_hbm.at[0], c_ref, 8),
         load(tt_hbm, tt_ref, 9),
@@ -154,12 +157,15 @@
     def keep_pencil(sb, rb, h):
         rb[me_p, pl.ds(h * HC, HC)] = sb[me_p, pl.ds(h * HC, HC)]
 
+    def place(d):
+        return lax.rem(d // 2, 2), 2 * (d // 4) + lax.rem(d, 2)
+
     def send_dp(e, sb, rb):
         @pl.loop(1, 16)
         def _(d):
             to = lax.rem(me_d + d, 16)
             pltpu.make_async_remote_copy(
-                src_ref=sb.at[to],
+                src_ref=sb.at[place(to)],
                 dst_ref=rb.at[me_d],
                 send_sem=ssem.at[e],
                 recv_sem=rsem.at[e],
@@ -167,7 +173,55 @@
                 device_id_type=MESH,
             ).start()
 
-        rb[me_d] = sb[me_d]
+        rb[me_d] = sb[place(me_d)]
+
+    def swap(i, src, dst):
+        return pltpu.make_async_remote_copy(
+            src_ref=src,
+            dst_ref=dst,
+            send_sem=yssem.at[i],
+            recv_sem=yrsem.at[i],
+            device_id=(partner, me_p),
+            device_id_type=MESH,
+        )
+
+    def piece(x, c):
+        return 2 * x + c
+
+    def part(r, half):
+        return wall.at[r, pl.ds(half * KH, KH)]
+
+    def weights(i, r, half, x, c):
+        return pltpu.make_async_remote_copy(
+            src_ref=part(r, half),
+            dst_ref=part(r, half),
+            send_sem=wssem.at[i],
+            recv_sem=wrsem.at[i],
+            device_id=(4 * x + 2 * me_y + c, me_p),
+            device_id_type=MESH,
+        )
+
+    sib = 1 - me_c
+    own, up, down, far = (piece(x, me_c) for x in (me_x, x_up, x_down, x_far))
+    moves = [
+        weights(0, own, 0, x_up, me_c),
+        weights(1, own, 1, x_down, me_c),
+        weights(2, own, 1, x_up, me_c),
+        weights(3, own, 0, x_down, me_c),
+        weights(4, own, 0, me_x, sib),
+        weights(5, own, 1, me_x, sib),
+        weights(6, down, 0, x_up, me_c),
+        weights(7, up, 1, x_down, me_c),
+        weights(8, down, 0, me_x, sib),
+        weights(9, up, 1, me_x, sib),
+        weights(10, down, 1, me_x, sib),
+        weights(11, up, 0, me_x, sib),
+        weights(12, far, 0, me_x, sib),
+        weights(13, far, 1, me_x, sib),
+    ]
+
+    def arrived(i):
+        moves[i].wait_recv()
 
     def wait_pencil(sem, buf, h):
         part = buf.at[pl.ds(0, 15), pl.ds(h * HC, HC)]
@@ -220,12 +274,12 @@
             zero = ((row % KH) == 0) & (lane < 64)
             turned = turned * jnp.where(zero, SCALE, 2.0 * SCALE)
         for j in range(16):
-            dst[j] = jnp.concatenate(
+            dst[(j // 2) % 2, 2 * (j // 4) + j % 2] = jnp.concatenate(
                 [turned[j * 8 : j * 8 + 8], turned[128 + j * 8 : 136 + j * 8]], axis=0
             ).astype(BF16)
 
     def modes_in(src):
-        v = [src[j].astype(F32) for j in range(16)]
+        v = [src[(j // 2) % 2, 2 * (j // 4) + j % 2].astype(F32) for j in range(16)]
         both = jnp.concatenate([t[:8] for t in v] + [t[8:] for t in v], axis=0)
         xi[...] = both.T.astype(BF16)
 
@@ -271,16 +325,14 @@
         if h == 0:
             pl.semaphore_wait(barrier, 30)
         send_pencil(h, s0, r0, h)
+        if h == 0:
+            loads[6].wait()
+            for i in range(6):
+                moves[i].start()
         keep_pencil(s0, r0, h)
 
-    loads[6].wait()
     loads[7].wait()
     lane64 = lax.broadcasted_iota(jnp.int32, (64, 128), 1)
-    for k in range(MZ):
-        w = w_ref[k].astype(F32)
-        turned = roll(w, 64)
-        turned = jnp.where(lane64 < 64, -turned, turned)
-        wb[k] = jnp.concatenate([w, turned], axis=0).astype(BF16)
     wl = wl_ref[...].astype(F32)
     wide = jnp.concatenate([wl] * 4, axis=1)
     tall = jnp.concatenate([wide] * 4, axis=0)
@@ -294,35 +346,83 @@
     for h in range(CHUNKS):
         wait_pencil(rsem.at[h], r0, h)
         x_forward(r0, h)
+        if h == 0:
+            arrived(0)
+            arrived(1)
+            for i in range(6, 10):
+                moves[i].start()
     modes_out(us, False)
-    send_dp(2, us, ur)
+    ask_u = swap(0, us.at[1 - me_y], row_u)
+    ask_u.start()
+    arrived(2)
+    arrived(3)
+    moves[10].start()
+    moves[11].start()
+    arrived(6)
+    arrived(7)
+    moves[12].start()
+    moves[13].start()
     loads[9].wait()
     loads[10].wait()
     loads[8].wait()
-    wait_dp(rsem.at[2], ur)
-
-    def regroup(src, i):
-        xf[...] = src[...].astype(F32).reshape(256, 128)
-        for k in range(KH):
-            re = xf[pl.ds(k, 16, stride=16), :]
-            im = xf[pl.ds(KH + k, 16, stride=16), :]
-            ukeep[i, k] = halves(re, roll(im, 64)).astype(BF16)
-            ukeep[i, KH + k] = halves(roll(re, 64), im).astype(BF16)
-
-    def products(mode, dst):
-        for k in range(KH):
-            low, high = mode(k), mode(KH + k)
-            vf[pl.ds(k, 16, stride=16), :] = halves(low, roll(high, 64))
-            vf[pl.ds(KH + k, 16, stride=16), :] = halves(roll(low, 64), high)
-        dst[...] = vf[...].astype(BF16).reshape(16, 16, 128)
-
-    regroup(ur, 0)
+
+    row16 = lax.broadcasted_iota(jnp.int32, (16, 128), 0)
+    lane16 = lax.broadcasted_iota(jnp.int32, (16, 128), 1)
+    block16 = [(row16 % KH) == (2 * t + lane16 // 64) for t in range(4)]
+    sign8 = jnp.where(lax.broadcasted_iota(jnp.int32, (8, 128), 1) < 64, -1.0, 1.0)
+    first8 = lax.broadcasted_iota(jnp.int32, (8, 128), 0) == 0
     root = math.sqrt(0.5)
-    products(lambda k: dot(ukeep[0, k], wb[k]) * (root * SCALE if k == 0 else 2.0 * root * SCALE), vs)
-    send_dp(3, vs, vr)
-    wait_dp(rsem.at[3], vr)
-
-    modes_in(vr)
+
+    def forward_mode(u, r):
+        u = u.astype(F32)
+        turned = roll(u, 64)
+        v = []
+        for kh in range(2):
+            twice = halves(u, turned) if kh == 0 else halves(turned, u)
+            lhs = jnp.concatenate([jnp.where(m, twice, 0.0) for m in block16], axis=1)
+            o = dot(lhs.astype(BF16), wall[r, kh * KH : (kh + 1) * KH].reshape(512, 128))
+            o = o[:8] + sign8 * roll(o[8:], 64)
+            scale = jnp.where(first8, root * SCALE, 2.0 * root * SCALE) if kh == 0 else 2.0 * root * SCALE
+            v.append(o * scale)
+        return jnp.concatenate(
+            [halves(v[0], roll(v[1], 64)), halves(roll(v[0], 64), v[1])], axis=0
+        ).astype(BF16)
+
+    def adjoint_mode(g, r):
+        g = g.astype(F32)
+        re, im = g[:8], g[8:]
+        re_t, im_t = roll(re, 64), roll(im, 64)
+        d = []
+        for kh in range(2):
+            if kh == 0:
+                lhs = [halves(re, im_t), halves(im, -re_t)]
+            else:
+                lhs = [halves(re_t, im), halves(im_t, -re)]
+            lhs = jnp.concatenate(lhs, axis=0).astype(BF16)
+            o = dot_t(lhs, wall[r, kh * KH : (kh + 1) * KH].reshape(512, 128))
+            o = sum(jnp.where(block16[t], o[:, t * 128 : (t + 1) * 128], 0.0) for t in range(4))
+            d.append(o + roll(o, 64))
+        return halves(d[0], d[1]).astype(BF16)
+
+    def local_modes(mode, src, dst, pieces):
+        for r in pieces:
+            dst[me_y, r] = mode(src[me_y, r], r)
+
+    def row_modes(mode, src, dst):
+        for r in range(8):
+            dst[r] = mode(src[r], r)
+
+    local_modes(forward_mode, us, row_v, (own, up, down, far))
+    for i in (4, 5, 8, 9, 10, 11, 12, 13):
+        arrived(i)
+    local_modes(forward_mode, us, row_v, [piece(x, sib) for x in (me_x, x_up, x_down, x_far)])
+    ask_u.wait_recv()
+    row_modes(forward_mode, row_u, back_v)
+    give_v = swap(1, back_v, row_v.at[me_y])
+    give_v.start()
+    send_dp(2, us, ur)
+    give_v.wait_recv()
+    modes_in(row_v)
     for h in range(CHUNKS):
         x_inverse(s1, h)
         send_pencil(4 + h, s1, r1, h)
@@ -368,23 +468,38 @@
         wait_pencil(rsem.at[6 + h], r2, h)
         x_forward(r2, h)
     modes_out(gs, True)
+    ask_g = swap(2, gs.at[1 - me_y], row_g)
+    ask_g.start()
+    local_modes(adjoint_mode, gs, row_d, range(8))
+    ask_g.wait_recv()
+    row_modes(adjoint_mode, row_g, back_d)
+    give_d = swap(3, back_d, row_d.at[me_y])
+    give_d.start()
     send_dp(8, gs, gr)
-    wait_dp(rsem.at[8], gr)
-
-    regroup(gr, 1)
-    products(lambda k: dot_t(ukeep[1, k], wb[k]), ds_)
-    send_dp(9, ds_, dr)
-    wait_dp(rsem.at[9], dr)
-
-    modes_in(dr)
-    own = []
+    give_d.wait_recv()
+    modes_in(row_d)
+    own_copies = []
     for h in range(CHUNKS):
         x_inverse(s3, h)
         send_pencil(10 + h, s3, r3, h)
-        part = pl.ds(h * HC, HC)
-        own.append(pltpu.make_async_copy(s3.at[me_p, part], r3.at[me_p, part], osem.at[2 + h]))
-        own[h].start()
-
+        rows = pl.ds(h * HC, HC)
+        own_copies.append(
+            pltpu.make_async_copy(s3.at[me_p, rows], r3.at[me_p, rows], osem.at[2 + h])
+        )
+        own_copies[h].start()
+
+    def regroup(src, i):
+        xf[...] = src[...].astype(F32).reshape(256, 128)
+        for k in range(KH):
+            re = xf[pl.ds(k, 16, stride=16), :]
+            im = xf[pl.ds(KH + k, 16, stride=16), :]
+            ukeep[i, k] = halves(re, roll(im, 64)).astype(BF16)
+            ukeep[i, KH + k] = halves(roll(re, 64), im).astype(BF16)
+
+    wait_dp(rsem.at[2], ur)
+    regroup(ur, 0)
+    wait_dp(rsem.at[8], gr)
+    regroup(gr, 1)
     for k in range(MZ):
         cross = lax.dot_general(
             ukeep[0, k], ukeep[1, k], (((0,), (0,)), ((), ())), preferred_element_type=F32
@@ -398,14 +513,14 @@
         wait_pencil(ssem.at[h], s0, h)
         wait_pencil(ssem.at[4 + h], s1, h)
         wait_pencil(ssem.at[6 + h], s2, h)
-    wait_dp(ssem.at[2], us)
-    wait_dp(ssem.at[3], vs)
-    wait_dp(ssem.at[8], gs)
-    wait_dp(ssem.at[9], ds_)
+    wait_dp(ssem.at[2], ur)
+    wait_dp(ssem.at[8], gr)
+    for copy in moves + [ask_u, give_v, ask_g, give_d]:
+        copy.wait_send()
     sp_copy.wait()
     gw_copy.wait()
     for h in range(CHUNKS):
-        own[h].wait()
+        own_copies[h].wait()
         wait_pencil(ssem.at[10 + h], s3, h)
         wait_pencil(rsem.at[10 + h], r3, h)
 
@@ -467,6 +582,8 @@
     any_spec = pl.BlockSpec(memory_space=pl.ANY)
     pencil_buf = pltpu.VMEM((16, CH, 128), BF16)
     dp_buf = pltpu.VMEM((16, 16, 128), BF16)
+    both = pltpu.VMEM((2, 8, 16, 128), BF16)
+    row = pltpu.VMEM((8, 16, 128), BF16)
     grid_b16 = pltpu.VMEM(grid, BF16)
     line = pltpu.VMEM((1024, 256), BF16)
     line_t = pltpu.VMEM((256, 1024), BF16)
@@ -483,7 +600,7 @@
         scratch_shapes=[
             grid_b16,
             grid_b16,
-            pltpu.VMEM((MZ, CH, 2 * CH), BF16),
+            pltpu.VMEM((8, MZ, CH, 2 * CH), BF16),
             pltpu.VMEM((CH, CH), BF16),
             line,
             line_t,
@@ -498,19 +615,21 @@
             pltpu.VMEM((8 * HC, 1024), BF16),
             pltpu.VMEM((128, 256), F32),
             pltpu.VMEM((128, 256), BF16),
-            pltpu.VMEM((MZ, 128, 128), BF16),
             pltpu.VMEM((2, 256, 256), BF16),
-            pltpu.VMEM((256, 128), F32),
             pltpu.VMEM((256, 128), F32),
             keep,
         ]
         + [pencil_buf] * 7
-        + [dp_buf] * 8
+        + [both, dp_buf, both, dp_buf, row, both, row, row, both, row]
         + [
             pltpu.SemaphoreType.DMA((11,)),
             pltpu.SemaphoreType.DMA((4,)),
             pltpu.SemaphoreType.DMA((12,)),
             pltpu.SemaphoreType.DMA((12,)),
+            pltpu.SemaphoreType.DMA((14,)),
+            pltpu.SemaphoreType.DMA((14,)),
+            pltpu.SemaphoreType.DMA((4,)),
+            pltpu.SemaphoreType.DMA((4,)),
         ],
         compiler_params=pltpu.CompilerParams(
             collective_id=0, has_side_effects=True, vmem_limit_bytes=60 * 1024 * 1024

time: 77.5 us -> 72.9 us (0.941)
  Pallas kernels: 76 us -> 72 us
    pallas_call x1, Pallas kernels: 71.3 us -> 67.2 us  [body(): pl.pallas_call(kernel, out_shape=(jax.ShapeDtypeStruct((16, CH, 128), BF1...]
where the time goes in v4:
time: 72.9 us; the launch traced here: 72.8 us
  Pallas kernels  72 us (99%)
  between operations  0.8 us (1%)
    pallas_call x1, Pallas kernels, body(): pl.pallas_call(kernel, out_shape=(jax.ShapeDtypeStruct((16, CH, 128), BF1...  67.2 us
    pallas_call x1, Pallas kernels, body(): pl.pallas_call(last_kernel, out_shape=(jax.ShapeDtypeStruct((1,) + grid,...  4.74 us

profile of v4, /device:TPU:8, one launch (start us, length us, event | category | flops | bytes accessed | tf_op | source)
XLA Modules:
  0.0 72.8 jit_solution(5588610513444135677)
XLA Ops:
  0.6 67.2 %layer.1 = (bf16[16,64,128]{2,1,0:T(8,128)(2,1)}, bf16[4,8,8,64,128]{4,3,2,1,0:T(8,128)(2,1)}, f32[16,64,128]{2,1,0:T(8,128)}) custom-call(bf16[1,4,8,8,64,128]{5,4,3,2,1,0:T(8,128)(2,1)} %bitcast.3, bf16[1,4,8,8,64,128]{5,4,3,2,1,0:T(8,128)(2,1)} %bitcast.4, bf16[1,1,16,64,128]{4,3,2,1,0:T(8,128)(2,1)} %w_hbm.1, bf16[64,64]{1,0:T(8,128)(2,1)} %wl_hbm.1, ...), custom_call_target="tpu_custom_call" | custom-call | tf_op jit(solution)/shard_map/layer/pallas_call | solution.py:591
  67.9 4.7 %last.1 = (bf16[1,4,8,8,64,128]{5,4,3,2,1,0:T(8,128)(2,1)}, f32[1,1,16,64,128]{4,3,2,1,0:T(8,128)}) custom-call(bf16[16,64,128]{2,1,0:T(8,128)(2,1)} %get-tuple-element.7.r_hbm, bf16[4,8,8,64,128]{4,3,2,1,0:T(8,128)(2,1)} %get-tuple-element.8.sp_hbm, f32[16,64,128]{2,1,0:T(8,128)} %get-tuple-element.9.gw_in, bf16[256,1024]{1,0:T(8,128)(2,1)} %constant.9.clone.tt_hbm, ...), custom_call_target="tpu_custom_call" | custom-call | tf_op jit(solution)/shard_map/last/pallas_call | solution.py:639

commit v5 on v4

--- a/solution.py
+++ b/solution.py
@@ -20,7 +20,7 @@
 MESH = pl.DeviceIdType.MESH
 F32 = jnp.float32
 BF16 = jnp.bfloat16
-CHUNKS = 2
+CHUNKS = 4
 HC = CH // CHUNKS
 SCALE = 1.0 / (NX * NY * NZ)
 
@@ -96,7 +96,7 @@
         at = (kh * 4 + x) * rows
         ly[at : at + rows, ri * 128 : (ri + 1) * 128] = tile.astype(BF16)
 
-    turn_slots(masks, lambda j: rb[j, c0 : c0 + rows, :].astype(F32), put)
+    turn_slots(masks, lambda j: rb[j, pl.ds(c0, rows), :].astype(F32), put)
 
 
 def kernel(
@@ -117,7 +117,18 @@
     def load(src, dst, i):
         return pltpu.make_async_copy(src, dst, lsem.at[i])
 
-    loads = [load(field_hbm.at[0, x], f_ref.at[x], x) for x in range(4)]
+    def rows_of(h):
+        return pl.ds(pl.multiple_of(h * HC, HC), HC)
+
+    every = slice(None)
+    loads = [
+        load(
+            field_hbm.at[0, every, every, every, rows_of(h)],
+            f_ref.at[every, every, every, rows_of(h)],
+            h,
+        )
+        for h in range(CHUNKS)
+    ]
     loads += [
         load(zf_hbm, zf_ref, 4),
         load(t_hbm, t_ref, 5),
@@ -127,7 +138,7 @@
         load(tt_hbm, tt_ref, 9),
         load(zt_hbm, zt_ref, 10),
     ]
-    for i in (4, 0, 1, 2, 3, 5, 6, 7, 9, 10, 8):
+    for i in (4, 0, 5, 6, 1, 2, 3, 7, 9, 10, 8):
         loads[i].start()
 
     barrier = pltpu.get_barrier_semaphore()
@@ -146,8 +157,8 @@
         def _(d):
             to = lax.rem(me_p + d, 16)
             pltpu.make_async_remote_copy(
-                src_ref=sb.at[to, pl.ds(h * HC, HC)],
-                dst_ref=rb.at[me_p, pl.ds(h * HC, HC)],
+                src_ref=sb.at[to, rows_of(h)],
+                dst_ref=rb.at[me_p, rows_of(h)],
                 send_sem=ssem.at[e],
                 recv_sem=rsem.at[e],
                 device_id=(me_d, to),
@@ -155,7 +166,7 @@
             ).start()
 
     def keep_pencil(sb, rb, h):
-        rb[me_p, pl.ds(h * HC, HC)] = sb[me_p, pl.ds(h * HC, HC)]
+        rb[me_p, rows_of(h)] = sb[me_p, rows_of(h)]
 
     def place(d):
         return lax.rem(d // 2, 2), 2 * (d // 4) + lax.rem(d, 2)
@@ -224,20 +235,21 @@
         moves[i].wait_recv()
 
     def wait_pencil(sem, buf, h):
-        part = buf.at[pl.ds(0, 15), pl.ds(h * HC, HC)]
+        part = buf.at[pl.ds(0, 15), rows_of(h)]
         pltpu.make_async_copy(part, part, sem).wait()
 
     def wait_dp(sem, buf):
         part = buf.at[pl.ds(0, 15)]
         pltpu.make_async_copy(part, part, sem).wait()
 
-    def z_store(a, x, g0, n):
-        for i in range(n):
-            for kh in range(2):
-                row = pl.multiple_of((kh * 4 + x) * HC, HC)
-                a2[pl.ds(row, HC), (g0 + i) * 128 : (g0 + i + 1) * 128] = a[
-                    i * HC : (i + 1) * HC, kh * 128 : (kh + 1) * 128
-                ]
+    def z_forward(parts):
+        a = dot(jnp.concatenate(parts, axis=1), zf_ref[...]).astype(BF16)
+        for x in range(4):
+            for g in range(8):
+                for kh in range(2):
+                    a2[(kh * 4 + x) * HC : (kh * 4 + x + 1) * HC, g * 128 : (g + 1) * 128] = a[
+                        (x * 8 + g) * HC : (x * 8 + g + 1) * HC, kh * 128 : (kh + 1) * 128
+                    ]
 
     def y_forward(sb, h):
         y = dot(a2[...], t_ref[...])
@@ -248,7 +260,7 @@
             return y[at : at + HC, ri * 128 : (ri + 1) * 128]
 
         def put(j, tile):
-            sb[j, h * HC : (h + 1) * HC, :] = tile.astype(BF16)
+            sb[j, rows_of(h), :] = tile.astype(BF16)
 
         turn_slots(slot_masks(HC), get, put)
 
@@ -283,16 +295,15 @@
         both = jnp.concatenate([t[:8] for t in v] + [t[8:] for t in v], axis=0)
         xi[...] = both.T.astype(BF16)
 
-    def x_inverse(sb, h):
-        lhs = jnp.concatenate(
-            [xi[kh * CH + h * HC : kh * CH + (h + 1) * HC, :] for kh in range(2)], axis=0
-        )
-        o = dot(lhs, tt_ref[...])
-        for g in range(8):
-            low = o[:HC, g * 128 : (g + 1) * 128]
-            high = o[HC:, g * 128 : (g + 1) * 128]
-            sb[2 * g, h * HC : (h + 1) * HC, :] = halves(low, roll(high, 64)).astype(BF16)
-            sb[2 * g + 1, h * HC : (h + 1) * HC, :] = halves(roll(low, 64), high).astype(BF16)
+    def x_inverse(sb, send):
+        o = dot(xi[...], tt_ref[...])
+        for h in range(CHUNKS):
+            for g in range(8):
+                low = o[h * HC : (h + 1) * HC, g * 128 : (g + 1) * 128]
+                high = o[CH + h * HC : CH + (h + 1) * HC, g * 128 : (g + 1) * 128]
+                sb[2 * g, h * HC : (h + 1) * HC, :] = halves(low, roll(high, 64)).astype(BF16)
+                sb[2 * g + 1, h * HC : (h + 1) * HC, :] = halves(roll(low, 64), high).astype(BF16)
+            send(h)
 
     def mix(lhs, src, dst, scale):
         @pl.loop(0, 4)
@@ -308,25 +319,21 @@
 
     loads[4].wait()
     for h in range(CHUNKS):
-        for x in range(4):
-            if h == 0:
-                loads[x].wait()
-            lhs = jnp.concatenate(
-                [
-                    f_ref[x, :, p, h * HC : (h + 1) * HC, :].reshape(8 * HC, 128)
-                    for p in range(8)
-                ],
-                axis=1,
-            )
-            z_store(dot(lhs, zf_ref[...]).astype(BF16), x, 0, 8)
+        loads[h].wait()
+        z_forward(
+            [
+                f_ref[:, :, p, h * HC : (h + 1) * HC, :].reshape(32 * HC, 128)
+                for p in range(8)
+            ]
+        )
         if h == 0:
             loads[5].wait()
         y_forward(s0, h)
         if h == 0:
+            loads[6].wait()
             pl.semaphore_wait(barrier, 30)
         send_pencil(h, s0, r0, h)
         if h == 0:
-            loads[6].wait()
             for i in range(6):
                 moves[i].start()
         keep_pencil(s0, r0, h)
@@ -343,14 +350,13 @@
     bw[1] = block.astype(BF16)
     mix(bw[0], f_ref, big, math.sqrt(0.5))
 
+    arrived(0)
+    arrived(1)
+    for i in range(6, 10):
+        moves[i].start()
     for h in range(CHUNKS):
         wait_pencil(rsem.at[h], r0, h)
         x_forward(r0, h)
-        if h == 0:
-            arrived(0)
-            arrived(1)
-            for i in range(6, 10):
-                moves[i].start()
     modes_out(us, False)
     ask_u = swap(0, us.at[1 - me_y], row_u)
     ask_u.start()
@@ -420,44 +426,44 @@
     row_modes(forward_mode, row_u, back_v)
     give_v = swap(1, back_v, row_v.at[me_y])
     give_v.start()
-    send_dp(2, us, ur)
+    send_dp(16, us, ur)
     give_v.wait_recv()
     modes_in(row_v)
+    x_inverse(s1, lambda h: send_pencil(4 + h, s1, r1, h))
     for h in range(CHUNKS):
-        x_inverse(s1, h)
-        send_pencil(4 + h, s1, r1, h)
         keep_pencil(s1, r1, h)
 
-    for h in range(CHUNKS):
+    @pl.loop(0, CHUNKS)
+    def _(h):
         wait_pencil(rsem.at[4 + h], r1, h)
-        y_inverse(r1, h * HC, HC, ly)
+        y_inverse(r1, pl.multiple_of(h * HC, HC), HC, ly)
         vy[...] = dot(ly[...], tt_ref[...]).astype(BF16)
-
-        @pl.loop(0, 2)
-        def _(x2, h=h):
-            for xi_ in range(2):
-                x = 2 * x2 + xi_
-                rows = [pl.ds(pl.multiple_of((kh * 4 + x) * HC, HC), HC) for kh in range(2)]
-                lhs = jnp.concatenate(
+        lhs = jnp.concatenate(
+            [
+                jnp.concatenate(
                     [
-                        jnp.concatenate([vy[r, g * 128 : (g + 1) * 128] for r in rows], axis=1)
-                        for g in range(8)
+                        vy[(kh * 4 + x) * HC : (kh * 4 + x + 1) * HC, g * 128 : (g + 1) * 128]
+                        for kh in range(2)
                     ],
-                    axis=0,
+                    axis=1,
                 )
-                parts = []
-                for n in range(4):
-                    v = dot(lhs, zt_ref[:, n * 256 : (n + 1) * 256])
-                    for i in range(2):
-                        at = (x, slice(None), 2 * n + i, slice(h * HC, (h + 1) * HC))
-                        pre = v[:, i * 128 : (i + 1) * 128].reshape(8, HC, 128) + big[at]
-                        sl = (c_ref[at].astype(F32) * gelu_slope(pre)).astype(BF16)
-                        slope[at] = sl
-                        parts.append(sl.reshape(8 * HC, 128))
-                z_store(dot(jnp.concatenate(parts, axis=1), zf_ref[...]).astype(BF16), x, 0, 8)
-
+                for x in range(4)
+                for g in range(8)
+            ],
+            axis=0,
+        )
+        parts = []
+        for n in range(4):
+            v = dot(lhs, zt_ref[:, n * 256 : (n + 1) * 256])
+            for i in range(2):
+                at = (every, every, 2 * n + i, rows_of(h))
+                t = v[:, i * 128 : (i + 1) * 128].reshape(4, 8, HC, 128) + big[at]
+                sl = (c_ref[at].astype(F32) * gelu_slope(t)).astype(BF16)
+                slope[at] = sl
+                parts.append(sl.reshape(32 * HC, 128))
+        z_forward(parts)
         y_forward(s2, h)
-        send_pencil(6 + h, s2, r2, h)
+        send_pencil(8 + h, s2, r2, h)
         keep_pencil(s2, r2, h)
 
     mix(bw[1], slope, sp, None)
@@ -465,7 +471,7 @@
     sp_copy.start()
 
     for h in range(CHUNKS):
-        wait_pencil(rsem.at[6 + h], r2, h)
+        wait_pencil(rsem.at[8 + h], r2, h)
         x_forward(r2, h)
     modes_out(gs, True)
     ask_g = swap(2, gs.at[1 - me_y], row_g)
@@ -475,18 +481,12 @@
     row_modes(adjoint_mode, row_g, back_d)
     give_d = swap(3, back_d, row_d.at[me_y])
     give_d.start()
-    send_dp(8, gs, gr)
+    send_dp(17, gs, gr)
     give_d.wait_recv()
     modes_in(row_d)
-    own_copies = []
-    for h in range(CHUNKS):
-        x_inverse(s3, h)
-        send_pencil(10 + h, s3, r3, h)
-        rows = pl.ds(h * HC, HC)
-        own_copies.append(
-            pltpu.make_async_copy(s3.at[me_p, rows], r3.at[me_p, rows], osem.at[2 + h])
-        )
-        own_copies[h].start()
+    x_inverse(s3, lambda h: send_pencil(12 + h, s3, r3, h))
+    own_copy = pltpu.make_async_copy(s3.at[me_p], r3.at[me_p], osem.at[2])
+    own_copy.start()
 
     def regroup(src, i):
         xf[...] = src[...].astype(F32).reshape(256, 128)
@@ -496,9 +496,9 @@
             ukeep[i, k] = halves(re, roll(im, 64)).astype(BF16)
             ukeep[i, KH + k] = halves(roll(re, 64), im).astype(BF16)
 
-    wait_dp(rsem.at[2], ur)
+    wait_dp(rsem.at[16], ur)
     regroup(ur, 0)
-    wait_dp(rsem.at[8], gr)
+    wait_dp(rsem.at[17], gr)
     regroup(gr, 1)
     for k in range(MZ):
         cross = lax.dot_general(
@@ -509,20 +509,20 @@
     gw_copy = pltpu.make_async_copy(gw_v, gw_hbm, osem.at[1])
     gw_copy.start()
 
+    for copy in moves + [ask_u, give_v, ask_g, give_d]:
+        copy.wait_send()
     for h in range(CHUNKS):
         wait_pencil(ssem.at[h], s0, h)
         wait_pencil(ssem.at[4 + h], s1, h)
-        wait_pencil(ssem.at[6 + h], s2, h)
-    wait_dp(ssem.at[2], ur)
-    wait_dp(ssem.at[8], gr)
-    for copy in moves + [ask_u, give_v, ask_g, give_d]:
-        copy.wait_send()
+        wait_pencil(ssem.at[8 + h], s2, h)
+    wait_dp(ssem.at[16], ur)
+    wait_dp(ssem.at[17], gr)
     sp_copy.wait()
     gw_copy.wait()
+    own_copy.wait()
     for h in range(CHUNKS):
-        own_copies[h].wait()
-        wait_pencil(ssem.at[10 + h], s3, h)
-        wait_pencil(rsem.at[10 + h], r3, h)
+        wait_pencil(ssem.at[12 + h], s3, h)
+        wait_pencil(rsem.at[12 + h], r3, h)
 
 
 def last_kernel(
@@ -624,8 +624,8 @@
         + [
             pltpu.SemaphoreType.DMA((11,)),
             pltpu.SemaphoreType.DMA((4,)),
-            pltpu.SemaphoreType.DMA((12,)),
-            pltpu.SemaphoreType.DMA((12,)),
+            pltpu.SemaphoreType.DMA((18,)),
+            pltpu.SemaphoreType.DMA((18,)),
             pltpu.SemaphoreType.DMA((14,)),
             pltpu.SemaphoreType.DMA((14,)),
             pltpu.SemaphoreType.DMA((4,)),

time: 72.9 us -> 70.9 us (0.973)
  Pallas kernels: 72 us -> 70 us
    pallas_call x1, Pallas kernels: 67.2 us -> 65.3 us  [body(): pl.pallas_call(kernel, out_shape=(jax.ShapeDtypeStruct((16, CH, 128), BF1...]
where the time goes in v5:
time: 70.9 us; the launch traced here: 70.6 us
  Pallas kernels  70 us (99%)
    pallas_call x1, Pallas kernels, body(): pl.pallas_call(kernel, out_shape=(jax.ShapeDtypeStruct((16, CH, 128), BF1...  65.3 us
    pallas_call x1, Pallas kernels, body(): pl.pallas_call(last_kernel, out_shape=(jax.ShapeDtypeStruct((1,) + grid,...  4.74 us

profile of v5, /device:TPU:8, one launch (start us, length us, event | category | flops | bytes accessed | tf_op | source)
XLA Modules:
  0.0 70.6 jit_solution(14080905229861801214)
XLA Ops:
  0.6 65.3 %layer.1 = (bf16[16,64,128]{2,1,0:T(8,128)(2,1)}, bf16[4,8,8,64,128]{4,3,2,1,0:T(8,128)(2,1)}, f32[16,64,128]{2,1,0:T(8,128)}) custom-call(bf16[1,4,8,8,64,128]{5,4,3,2,1,0:T(8,128)(2,1)} %bitcast.3, bf16[1,4,8,8,64,128]{5,4,3,2,1,0:T(8,128)(2,1)} %bitcast.4, bf16[1,1,16,64,128]{4,3,2,1,0:T(8,128)(2,1)} %w_hbm.1, bf16[64,64]{1,0:T(8,128)(2,1)} %wl_hbm.1, ...), custom_call_target="tpu_custom_call" | custom-call | tf_op jit(solution)/shard_map/layer/pallas_call | solution.py:591
  65.9 4.7 %last.1 = (bf16[1,4,8,8,64,128]{5,4,3,2,1,0:T(8,128)(2,1)}, f32[1,1,16,64,128]{4,3,2,1,0:T(8,128)}) custom-call(bf16[16,64,128]{2,1,0:T(8,128)(2,1)} %get-tuple-element.7.r_hbm, bf16[4,8,8,64,128]{4,3,2,1,0:T(8,128)(2,1)} %get-tuple-element.8.sp_hbm, f32[16,64,128]{2,1,0:T(8,128)} %get-tuple-element.9.gw_in, bf16[256,1024]{1,0:T(8,128)(2,1)} %constant.9.clone.tt_hbm, ...), custom_call_target="tpu_custom_call" | custom-call | tf_op jit(solution)/shard_map/last/pallas_call | solution.py:639

commit v6 on v5

--- a/solution.py
+++ b/solution.py
@@ -101,12 +101,12 @@
 
 def kernel(
     field_hbm, cot_hbm, w_hbm, wl_hbm, t_hbm, tt_hbm, zf_hbm, zt_hbm,
-    r3, sp_hbm, gw_hbm,
-    f_ref, c_ref, wall, wl_ref, t_ref, tt_ref, zf_ref, zt_ref, big, slope, sp, gw_v,
+    r3, sp, gw_v, tt_ref, zt_ref,
+    f_ref, c_ref, wall, wl_ref, t_ref, zf_ref, big, slope,
     a2, ly, vy, xo, xi, bw, xf, ukeep,
     s0, r0, s1, r1, s2, r2, s3,
     us, ur, gs, gr, row_u, row_v, back_v, row_g, row_d, back_d,
-    lsem, osem, ssem, rsem, wssem, wrsem, yssem, yrsem,
+    lsem, ssem, rsem, wssem, wrsem, yssem, yrsem,
 ):
     me_d = lax.axis_index("dp")
     me_p = lax.axis_index("pencil")
@@ -467,8 +467,6 @@
         keep_pencil(s2, r2, h)
 
     mix(bw[1], slope, sp, None)
-    sp_copy = pltpu.make_async_copy(sp, sp_hbm, osem.at[0])
-    sp_copy.start()
 
     for h in range(CHUNKS):
         wait_pencil(rsem.at[8 + h], r2, h)
@@ -485,8 +483,7 @@
     give_d.wait_recv()
     modes_in(row_d)
     x_inverse(s3, lambda h: send_pencil(12 + h, s3, r3, h))
-    own_copy = pltpu.make_async_copy(s3.at[me_p], r3.at[me_p], osem.at[2])
-    own_copy.start()
+    r3[me_p] = s3[me_p]
 
     def regroup(src, i):
         xf[...] = src[...].astype(F32).reshape(256, 128)
@@ -506,8 +503,6 @@
         )
         low = roll(cross[64:], 64)
         gw_v[k] = cross[:64] + jnp.where(lane64 < 64, low, -low)
-    gw_copy = pltpu.make_async_copy(gw_v, gw_hbm, osem.at[1])
-    gw_copy.start()
 
     for copy in moves + [ask_u, give_v, ask_g, give_d]:
         copy.wait_send()
@@ -517,35 +512,20 @@
         wait_pencil(ssem.at[8 + h], s2, h)
     wait_dp(ssem.at[16], ur)
     wait_dp(ssem.at[17], gr)
-    sp_copy.wait()
-    gw_copy.wait()
-    own_copy.wait()
     for h in range(CHUNKS):
         wait_pencil(ssem.at[12 + h], s3, h)
         wait_pencil(rsem.at[12 + h], r3, h)
 
 
 def last_kernel(
-    r_hbm, sp_hbm, gw_in, tt_hbm, zt_hbm, out_hbm, gw_hbm,
-    r_ref, sp, tt_ref, zt_ref, ly, vy, out_v, gw_v, lsem, osem,
+    r_ref, sp, gw_v, tt_ref, zt_ref, out_hbm, gw_hbm, ly, vy, out_v, osem,
 ):
-    loads = [
-        pltpu.make_async_copy(r_hbm, r_ref, lsem.at[0]),
-        pltpu.make_async_copy(tt_hbm, tt_ref, lsem.at[1]),
-        pltpu.make_async_copy(zt_hbm, zt_ref, lsem.at[2]),
-        pltpu.make_async_copy(gw_in, gw_v, lsem.at[3]),
-    ]
-    loads += [pltpu.make_async_copy(sp_hbm.at[x], sp.at[x], lsem.at[4 + x]) for x in range(4)]
-    for copy in loads:
-        copy.start()
-    loads[0].wait()
+    gw_copy = pltpu.make_async_copy(gw_v, gw_hbm.at[0, 0], osem.at[4])
+    gw_copy.start()
     y_inverse(r_ref, 0, CH, ly)
-    loads[1].wait()
     vy[...] = dot(ly[...], tt_ref[...]).astype(BF16)
-    loads[2].wait()
     outs = []
     for x in range(4):
-        loads[4 + x].wait()
         lhs = jnp.concatenate(
             [
                 jnp.concatenate(
@@ -566,20 +546,17 @@
                 out_v[x, :, 2 * n + i] = (part + sp[x, :, 2 * n + i].astype(F32)).astype(BF16)
         outs.append(pltpu.make_async_copy(out_v.at[x], out_hbm.at[0, x], osem.at[x]))
         outs[x].start()
-        if x == 0:
-            loads[3].wait()
-            outs_gw = pltpu.make_async_copy(gw_v, gw_hbm.at[0, 0], osem.at[4])
-            outs_gw.start()
     for copy in outs:
         copy.wait()
-    outs_gw.wait()
+    gw_copy.wait()
 
 
 def body(field, cotangent, w_spec, w_local):
     table, zf = line_table(), z_table()
     t, tt, zf, zt = (jnp.asarray(m.astype(jnp.bfloat16)) for m in (table, table.T, zf, zf.T))
     grid = (4, 8, 8, CH, NZ)
-    any_spec = pl.BlockSpec(memory_space=pl.ANY)
+    any_spec = pl.BlockSpec(memory_space=pltpu.HBM)
+    vmem_spec = pl.BlockSpec(memory_space=pltpu.VMEM)
     pencil_buf = pltpu.VMEM((16, CH, 128), BF16)
     dp_buf = pltpu.VMEM((16, 16, 128), BF16)
     both = pltpu.VMEM((2, 8, 16, 128), BF16)
@@ -588,28 +565,26 @@
     line = pltpu.VMEM((1024, 256), BF16)
     line_t = pltpu.VMEM((256, 1024), BF16)
     keep = pltpu.VMEM((2, MZ, 16, 128), BF16)
-    r3, sp, gw = pl.pallas_call(
+    r3, sp, gw, tt, zt = pl.pallas_call(
         kernel,
         out_shape=(
-            jax.ShapeDtypeStruct((16, CH, 128), BF16),
-            jax.ShapeDtypeStruct(grid, BF16),
-            jax.ShapeDtypeStruct((MZ, CH, 2 * CH), F32),
+            pencil_buf,
+            grid_b16,
+            pltpu.VMEM((MZ, CH, 2 * CH), F32),
+            line_t,
+            line_t,
         ),
         in_specs=[any_spec] * 8,
-        out_specs=[any_spec] * 3,
+        out_specs=[vmem_spec] * 5,
         scratch_shapes=[
             grid_b16,
             grid_b16,
             pltpu.VMEM((8, MZ, CH, 2 * CH), BF16),
             pltpu.VMEM((CH, CH), BF16),
             line,
-            line_t,
             line,
-            line_t,
             pltpu.VMEM(grid, F32),
             grid_b16,
-            grid_b16,
-            pltpu.VMEM((MZ, CH, 2 * CH), F32),
             pltpu.VMEM((8 * HC, 1024), BF16),
             pltpu.VMEM((8 * HC, 256), BF16),
             pltpu.VMEM((8 * HC, 1024), BF16),
@@ -623,7 +598,6 @@
         + [both, dp_buf, both, dp_buf, row, both, row, row, both, row]
         + [
             pltpu.SemaphoreType.DMA((11,)),
-            pltpu.SemaphoreType.DMA((4,)),
             pltpu.SemaphoreType.DMA((18,)),
             pltpu.SemaphoreType.DMA((18,)),
             pltpu.SemaphoreType.DMA((14,)),
@@ -632,7 +606,7 @@
             pltpu.SemaphoreType.DMA((4,)),
         ],
         compiler_params=pltpu.CompilerParams(
-            collective_id=0, has_side_effects=True, vmem_limit_bytes=60 * 1024 * 1024
+            collective_id=0, has_side_effects=True, vmem_limit_bytes=60_900_000
         ),
         name="layer",
     )(field.reshape((1,) + grid), cotangent.reshape((1,) + grid), w_spec, w_local, t, tt, zf, zt)
@@ -642,21 +616,15 @@
             jax.ShapeDtypeStruct((1,) + grid, BF16),
             jax.ShapeDtypeStruct((1, 1, MZ, CH, 2 * CH), F32),
         ),
-        in_specs=[any_spec] * 5,
+        in_specs=[vmem_spec] * 5,
         out_specs=[any_spec] * 2,
         scratch_shapes=[
-            pencil_buf,
-            grid_b16,
-            line_t,
-            line_t,
             pltpu.VMEM((8 * CH, 256), BF16),
             pltpu.VMEM((8 * CH, 1024), BF16),
             grid_b16,
-            pltpu.VMEM((MZ, CH, 2 * CH), F32),
-            pltpu.SemaphoreType.DMA((8,)),
             pltpu.SemaphoreType.DMA((5,)),
         ],
-        compiler_params=pltpu.CompilerParams(vmem_limit_bytes=60 * 1024 * 1024),
+        compiler_params=pltpu.CompilerParams(vmem_limit_bytes=20 * 1024 * 1024),
         name="last",
     )(r3, sp, gw, tt, zt)
     return (out.reshape(1, 4, NY, CH, NZ), gw)

time: 70.9 us -> 69.1 us (0.975)
  Pallas kernels: 70 us -> 68.4 us
    pallas_call x1, Pallas kernels: 4.74 us -> 3.12 us  [body(): pl.pallas_call(last_kernel, out_shape=(jax.ShapeDtypeStruct((1,) + grid,...]
where the time goes in v6:
time: 69.1 us; the launch traced here: 69 us
  Pallas kernels  68.4 us (99%)
    pallas_call x1, Pallas kernels, body(): pl.pallas_call(kernel, out_shape=(pencil_buf, grid_b16, pltpu.VMEM((MZ, C...  65.3 us
    pallas_call x1, Pallas kernels, body(): pl.pallas_call(last_kernel, out_shape=(jax.ShapeDtypeStruct((1,) + grid,...  3.12 us

profile of v6, /device:TPU:8, one launch (start us, length us, event | category | flops | bytes accessed | tf_op | source)
XLA Modules:
  0.0 69.0 jit_solution(11496616124763750601)
XLA Ops:
  0.6 65.3 %layer.1 = (bf16[16,64,128]{2,1,0:T(8,128)(2,1)S(1)}, bf16[4,8,8,64,128]{4,3,2,1,0:T(8,128)(2,1)S(1)}, f32[16,64,128]{2,1,0:T(8,128)S(1)}, bf16[256,1024]{1,0:T(8,128)(2,1)S(1)}, bf16[256,1024]{1,0:T(8,128)(2,1)S(1)}) custom-call(bf16[1,4,8,8,64,128]{5,4,3,2,1,0:T(8,128)(2,1)} %bitcast.3, bf16[1,4,8,8,64,128]{5,4,3,2,1,0:T(8,128)(2,1)} %bitcast.4, ...), custom_call_target="tpu_custom_call" | custom-call | tf_op jit(solution)/shard_map/layer/pallas_call | solution.py:568
  65.9 3.1 %last.1 = (bf16[1,4,8,8,64,128]{5,4,3,2,1,0:T(8,128)(2,1)}, f32[1,1,16,64,128]{4,3,2,1,0:T(8,128)}) custom-call(bf16[16,64,128]{2,1,0:T(8,128)(2,1)S(1)} %get-tuple-element.9.r_ref, bf16[4,8,8,64,128]{4,3,2,1,0:T(8,128)(2,1)S(1)} %get-tuple-element.10.sp, f32[16,64,128]{2,1,0:T(8,128)S(1)} %get-tuple-element.11.gw_v, ...), custom_call_target="tpu_custom_call" | custom-call | tf_op jit(solution)/shard_map/last/pallas_call | solution.py:613

commit v7 on v6

--- a/solution.py
+++ b/solution.py
@@ -59,9 +59,9 @@
     return lax.dot_general(a, b, (((1,), (1,)), ((), ())), preferred_element_type=F32)
 
 
-def gelu_slope(t):
-    bell = jnp.exp2(t * t * (-1.0 / math.log(2.0)) - 0.5 * math.log2(math.pi))
-    return 0.5 * lax.erf(t) + (t * bell + 0.5)
+def gelu_slope_twice(t):
+    bell = jnp.exp2(t * t * (-1.0 / math.log(2.0)) + math.log2(2.0 / math.sqrt(math.pi)))
+    return lax.erf(t) + (t * bell + 1.0)
 
 
 def roll(v, amount):
@@ -153,8 +153,7 @@
         )
 
     def send_pencil(e, sb, rb, h):
-        @pl.loop(1, 16)
-        def _(d):
+        for d in (8, 7, 9, 6, 10, 5, 11, 4, 12, 3, 13, 2, 14, 1, 15):
             to = lax.rem(me_p + d, 16)
             pltpu.make_async_remote_copy(
                 src_ref=sb.at[to, rows_of(h)],
@@ -284,7 +283,7 @@
             row = lax.broadcasted_iota(jnp.int32, (256, 128), 0)
             lane = lax.broadcasted_iota(jnp.int32, (256, 128), 1)
             zero = ((row % KH) == 0) & (lane < 64)
-            turned = turned * jnp.where(zero, SCALE, 2.0 * SCALE)
+            turned = turned * jnp.where(zero, 0.5 * SCALE, SCALE)
         for j in range(16):
             dst[(j // 2) % 2, 2 * (j // 4) + j % 2] = jnp.concatenate(
                 [turned[j * 8 : j * 8 + 8], turned[128 + j * 8 : 136 + j * 8]], axis=0
@@ -305,8 +304,8 @@
                 sb[2 * g + 1, h * HC : (h + 1) * HC, :] = halves(roll(low, 64), high).astype(BF16)
             send(h)
 
-    def mix(lhs, src, dst, scale):
-        @pl.loop(0, 4)
+    def mix(lhs, src, dst, scale, first, last):
+        @pl.loop(first, last)
         def _(x):
             for g in range(8):
                 rhs = jnp.concatenate(
@@ -347,13 +346,14 @@
     col = lax.broadcasted_iota(jnp.int32, (256, 256), 1) // 64
     block = jnp.where(row == col, tall, 0.0)
     bw[0] = block.T.astype(BF16)
-    bw[1] = block.astype(BF16)
-    mix(bw[0], f_ref, big, math.sqrt(0.5))
-
+    bw[1] = (0.5 * block).astype(BF16)
+    mix(bw[0], f_ref, big, math.sqrt(0.5), 0, 2)
     arrived(0)
     arrived(1)
     for i in range(6, 10):
         moves[i].start()
+    mix(bw[0], f_ref, big, math.sqrt(0.5), 2, 4)
+
     for h in range(CHUNKS):
         wait_pencil(rsem.at[h], r0, h)
         x_forward(r0, h)
@@ -421,11 +421,11 @@
     local_modes(forward_mode, us, row_v, (own, up, down, far))
     for i in (4, 5, 8, 9, 10, 11, 12, 13):
         arrived(i)
-    local_modes(forward_mode, us, row_v, [piece(x, sib) for x in (me_x, x_up, x_down, x_far)])
     ask_u.wait_recv()
     row_modes(forward_mode, row_u, back_v)
     give_v = swap(1, back_v, row_v.at[me_y])
     give_v.start()
+    local_modes(forward_mode, us, row_v, [piece(x, sib) for x in (me_x, x_up, x_down, x_far)])
     send_dp(16, us, ur)
     give_v.wait_recv()
     modes_in(row_v)
@@ -458,7 +458,7 @@
             for i in range(2):
                 at = (every, every, 2 * n + i, rows_of(h))
                 t = v[:, i * 128 : (i + 1) * 128].reshape(4, 8, HC, 128) + big[at]
-                sl = (c_ref[at].astype(F32) * gelu_slope(t)).astype(BF16)
+                sl = (c_ref[at].astype(F32) * gelu_slope_twice(t)).astype(BF16)
                 slope[at] = sl
                 parts.append(sl.reshape(32 * HC, 128))
         z_forward(parts)
@@ -466,7 +466,7 @@
         send_pencil(8 + h, s2, r2, h)
         keep_pencil(s2, r2, h)
 
-    mix(bw[1], slope, sp, None)
+    mix(bw[1], slope, sp, None, 0, 4)
 
     for h in range(CHUNKS):
         wait_pencil(rsem.at[8 + h], r2, h)

time: 69.1 us -> 66.8 us (0.967)
  Pallas kernels: 68.4 us -> 65.8 us
    pallas_call x1, Pallas kernels: 65.3 us -> 62.7 us  [body(): pl.pallas_call(kernel, out_shape=(pencil_buf, grid_b16, pltpu.VMEM((MZ, C...]
where the time goes in v7:
time: 66.8 us; the launch traced here: 66.5 us
  Pallas kernels  65.8 us (99%)
    pallas_call x1, Pallas kernels, body(): pl.pallas_call(kernel, out_shape=(pencil_buf, grid_b16, pltpu.VMEM((MZ, C...  62.7 us
    pallas_call x1, Pallas kernels, body(): pl.pallas_call(last_kernel, out_shape=(jax.ShapeDtypeStruct((1,) + grid,...  3.12 us

profile of v7, /device:TPU:8, one launch (start us, length us, event | category | flops | bytes accessed | tf_op | source)
XLA Modules:
  0.0 66.5 jit_solution(17834150897790878721)
XLA Ops:
  0.6 62.7 %layer.1 = (bf16[16,64,128]{2,1,0:T(8,128)(2,1)S(1)}, bf16[4,8,8,64,128]{4,3,2,1,0:T(8,128)(2,1)S(1)}, f32[16,64,128]{2,1,0:T(8,128)S(1)}, bf16[256,1024]{1,0:T(8,128)(2,1)S(1)}, bf16[256,1024]{1,0:T(8,128)(2,1)S(1)}) custom-call(bf16[1,4,8,8,64,128]{5,4,3,2,1,0:T(8,128)(2,1)} %bitcast.3, bf16[1,4,8,8,64,128]{5,4,3,2,1,0:T(8,128)(2,1)} %bitcast.4, ...), custom_call_target="tpu_custom_call" | custom-call | tf_op jit(solution)/shard_map/layer/pallas_call | solution.py:568
  63.4 3.1 %last.1 = (bf16[1,4,8,8,64,128]{5,4,3,2,1,0:T(8,128)(2,1)}, f32[1,1,16,64,128]{4,3,2,1,0:T(8,128)}) custom-call(bf16[16,64,128]{2,1,0:T(8,128)(2,1)S(1)} %get-tuple-element.9.r_ref, bf16[4,8,8,64,128]{4,3,2,1,0:T(8,128)(2,1)S(1)} %get-tuple-element.10.sp, f32[16,64,128]{2,1,0:T(8,128)S(1)} %get-tuple-element.11.gw_v, ...), custom_call_target="tpu_custom_call" | custom-call | tf_op jit(solution)/shard_map/last/pallas_call | solution.py:613

commit v8 on v7

--- a/solution.py
+++ b/solution.py
@@ -99,9 +99,36 @@
     turn_slots(masks, lambda j: rb[j, pl.ds(c0, rows), :].astype(F32), put)
 
 
+def grid_modes(ly, vy, tt_ref):
+    vy[...] = dot(ly[...], tt_ref[...]).astype(BF16)
+    return jnp.concatenate(
+        [
+            jnp.concatenate(
+                [
+                    vy[(kh * 4 + x) * HC : (kh * 4 + x + 1) * HC, g * 128 : (g + 1) * 128]
+                    for kh in range(2)
+                ],
+                axis=1,
+            )
+            for x in range(4)
+            for g in range(8)
+        ],
+        axis=0,
+    )
+
+
+def finish(lhs, zt_ref, sp, dst, c_from, c_to):
+    for n in range(4):
+        v = dot(lhs, zt_ref[:, n * 256 : (n + 1) * 256])
+        for i in range(2):
+            p = 2 * n + i
+            part = v[:, i * 128 : (i + 1) * 128].reshape(4, 8, HC, 128)
+            dst[:, :, p, c_to] = (part + sp[:, :, p, c_from].astype(F32)).astype(BF16)
+
+
 def kernel(
     field_hbm, cot_hbm, w_hbm, wl_hbm, t_hbm, tt_hbm, zf_hbm, zt_hbm,
-    r3, sp, gw_v, tt_ref, zt_ref,
+    r3, sp, gw_v, tt_ref, zt_ref, out_v,
     f_ref, c_ref, wall, wl_ref, t_ref, zf_ref, big, slope,
     a2, ly, vy, xo, xi, bw, xf, ukeep,
     s0, r0, s1, r1, s2, r2, s3,
@@ -437,21 +464,7 @@
     def _(h):
         wait_pencil(rsem.at[4 + h], r1, h)
         y_inverse(r1, pl.multiple_of(h * HC, HC), HC, ly)
-        vy[...] = dot(ly[...], tt_ref[...]).astype(BF16)
-        lhs = jnp.concatenate(
-            [
-                jnp.concatenate(
-                    [
-                        vy[(kh * 4 + x) * HC : (kh * 4 + x + 1) * HC, g * 128 : (g + 1) * 128]
-                        for kh in range(2)
-                    ],
-                    axis=1,
-                )
-                for x in range(4)
-                for g in range(8)
-            ],
-            axis=0,
-        )
+        lhs = grid_modes(ly, vy, tt_ref)
         parts = []
         for n in range(4):
             v = dot(lhs, zt_ref[:, n * 256 : (n + 1) * 256])
@@ -504,6 +517,12 @@
         low = roll(cross[64:], 64)
         gw_v[k] = cross[:64] + jnp.where(lane64 < 64, low, -low)
 
+    @pl.loop(0, CHUNKS - 1)
+    def _(h):
+        wait_pencil(rsem.at[12 + h], r3, h)
+        y_inverse(r3, pl.multiple_of(h * HC, HC), HC, ly)
+        finish(grid_modes(ly, vy, tt_ref), zt_ref, sp, out_v, rows_of(h), rows_of(h))
+
     for copy in moves + [ask_u, give_v, ask_g, give_d]:
         copy.wait_send()
     for h in range(CHUNKS):
@@ -514,41 +533,32 @@
     wait_dp(ssem.at[17], gr)
     for h in range(CHUNKS):
         wait_pencil(ssem.at[12 + h], s3, h)
-        wait_pencil(rsem.at[12 + h], r3, h)
+    wait_pencil(rsem.at[12 + CHUNKS - 1], r3, CHUNKS - 1)
 
 
 def last_kernel(
-    r_ref, sp, gw_v, tt_ref, zt_ref, out_hbm, gw_hbm, ly, vy, out_v, osem,
+    r_ref, sp, gw_v, tt_ref, zt_ref, done, out_hbm, gw_hbm, ly, vy, out_v, osem,
 ):
-    gw_copy = pltpu.make_async_copy(gw_v, gw_hbm.at[0, 0], osem.at[4])
-    gw_copy.start()
-    y_inverse(r_ref, 0, CH, ly)
-    vy[...] = dot(ly[...], tt_ref[...]).astype(BF16)
-    outs = []
-    for x in range(4):
-        lhs = jnp.concatenate(
-            [
-                jnp.concatenate(
-                    [
-                        vy[(kh * 4 + x) * CH : (kh * 4 + x + 1) * CH, g * 128 : (g + 1) * 128]
-                        for kh in range(2)
-                    ],
-                    axis=1,
-                )
-                for g in range(8)
-            ],
-            axis=0,
-        )
-        for n in range(4):
-            v = dot(lhs, zt_ref[:, n * 256 : (n + 1) * 256])
-            for i in range(2):
-                part = v[:, i * 128 : (i + 1) * 128].reshape(8, CH, 128)
-                out_v[x, :, 2 * n + i] = (part + sp[x, :, 2 * n + i].astype(F32)).astype(BF16)
-        outs.append(pltpu.make_async_copy(out_v.at[x], out_hbm.at[0, x], osem.at[x]))
-        outs[x].start()
-    for copy in outs:
+    every, rest = slice(None), CH - HC
+    copies = [
+        pltpu.make_async_copy(
+            done.at[x], out_hbm.at[0, x, every, every, pl.ds(0, rest)], osem.at[x]
+        )
+        for x in range(4)
+    ]
+    copies.append(pltpu.make_async_copy(gw_v, gw_hbm.at[0, 0], osem.at[4]))
+    for copy in copies:
+        copy.start()
+    y_inverse(r_ref, rest, HC, ly)
+    finish(grid_modes(ly, vy, tt_ref), zt_ref, sp, out_v, pl.ds(rest, HC), pl.ds(0, HC))
+    copies.append(
+        pltpu.make_async_copy(
+            out_v, out_hbm.at[0, every, every, every, pl.ds(rest, HC)], osem.at[5]
+        )
+    )
+    copies[5].start()
+    for copy in copies:
         copy.wait()
-    gw_copy.wait()
 
 
 def body(field, cotangent, w_spec, w_local):
@@ -565,7 +575,7 @@
     line = pltpu.VMEM((1024, 256), BF16)
     line_t = pltpu.VMEM((256, 1024), BF16)
     keep = pltpu.VMEM((2, MZ, 16, 128), BF16)
-    r3, sp, gw, tt, zt = pl.pallas_call(
+    r3, sp, gw, tt, zt, done = pl.pallas_call(
         kernel,
         out_shape=(
             pencil_buf,
@@ -573,9 +583,10 @@
             pltpu.VMEM((MZ, CH, 2 * CH), F32),
             line_t,
             line_t,
+            pltpu.VMEM((4, 8, 8, CH - HC, NZ), BF16),
         ),
         in_specs=[any_spec] * 8,
-        out_specs=[vmem_spec] * 5,
+        out_specs=[vmem_spec] * 6,
         scratch_shapes=[
             grid_b16,
             grid_b16,
@@ -606,7 +617,7 @@
             pltpu.SemaphoreType.DMA((4,)),
         ],
         compiler_params=pltpu.CompilerParams(
-            collective_id=0, has_side_effects=True, vmem_limit_bytes=60_900_000
+            collective_id=0, has_side_effects=True, vmem_limit_bytes=57_700_000
         ),
         name="layer",
     )(field.reshape((1,) + grid), cotangent.reshape((1,) + grid), w_spec, w_local, t, tt, zf, zt)
@@ -616,17 +627,17 @@
             jax.ShapeDtypeStruct((1,) + grid, BF16),
             jax.ShapeDtypeStruct((1, 1, MZ, CH, 2 * CH), F32),
         ),
-        in_specs=[vmem_spec] * 5,
+        in_specs=[vmem_spec] * 6,
         out_specs=[any_spec] * 2,
         scratch_shapes=[
-            pltpu.VMEM((8 * CH, 256), BF16),
-            pltpu.VMEM((8 * CH, 1024), BF16),
-            grid_b16,
-            pltpu.SemaphoreType.DMA((5,)),
+            pltpu.VMEM((8 * HC, 256), BF16),
+            pltpu.VMEM((8 * HC, 1024), BF16),
+            pltpu.VMEM((4, 8, 8, HC, NZ), BF16),
+            pltpu.SemaphoreType.DMA((6,)),
         ],
         compiler_params=pltpu.CompilerParams(vmem_limit_bytes=20 * 1024 * 1024),
         name="last",
-    )(r3, sp, gw, tt, zt)
+    )(r3, sp, gw, tt, zt, done)
     return (out.reshape(1, 4, NY, CH, NZ), gw)
 
 

time: 66.8 us -> 66.5 us (level)
    pallas_call x1, Pallas kernels: 3.12 us -> 2.39 us  [body(): pl.pallas_call(last_kernel, out_shape=(jax.ShapeDtypeStruct((1,) + grid,...]
where the time goes in v8:
time: 66.5 us; the launch traced here: 66.2 us
  Pallas kernels  65.6 us (99%)
    pallas_call x1, Pallas kernels, body(): pl.pallas_call(kernel, out_shape=(pencil_buf, grid_b16, pltpu.VMEM((MZ, C...  63.2 us
    pallas_call x1, Pallas kernels, body(): pl.pallas_call(last_kernel, out_shape=(jax.ShapeDtypeStruct((1,) + grid,...  2.39 us

profile of v8, /device:TPU:8, one launch (start us, length us, event | category | flops | bytes accessed | tf_op | source)
XLA Modules:
  0.0 66.2 jit_solution(14310134783155524667)
XLA Ops:
  0.6 63.2 %layer.1 = (bf16[16,64,128]{2,1,0:T(8,128)(2,1)S(1)}, bf16[4,8,8,64,128]{4,3,2,1,0:T(8,128)(2,1)S(1)}, f32[16,64,128]{2,1,0:T(8,128)S(1)}, bf16[256,1024]{1,0:T(...) custom-call(bf16[1,4,8,8,64,128]{5,4,3,2,1,0:T(8,128)(2,1)} %bitcast.3, ...), custom_call_target="tpu_custom_call" | custom-call | tf_op jit(solution)/shard_map/layer/pallas_call | solution.py:578
  63.8 2.4 %last.1 = (bf16[1,4,8,8,64,128]{5,4,3,2,1,0:T(8,128)(2,1)}, f32[1,1,16,64,128]{4,3,2,1,0:T(8,128)}) custom-call(bf16[16,64,128]{2,1,0:T(8,128)(2,1)S(1)} %get-tuple-element.10.r_ref, bf16[4,8,8,64,128]{4,3,2,1,0:T(8,128)(2,1)S(1)} %get-tuple-element.11.sp, f32[16,64,128]{2,1,0:T(8,128)S(1)} %get-tuple-element.12.gw_v, ...), custom_call_target="tpu_custom_call" | custom-call | tf_op jit(solution)/shard_map/last/pallas_call | solution.py:624

commit v9 on v8

--- a/solution.py
+++ b/solution.py
@@ -22,6 +22,7 @@
 BF16 = jnp.bfloat16
 CHUNKS = 4
 HC = CH // CHUNKS
+EARLY = 2
 SCALE = 1.0 / (NX * NY * NZ)
 
 
@@ -384,13 +385,14 @@
     for h in range(CHUNKS):
         wait_pencil(rsem.at[h], r0, h)
         x_forward(r0, h)
+        if h == 1:
+            arrived(2)
+            arrived(3)
+            moves[10].start()
+            moves[11].start()
     modes_out(us, False)
     ask_u = swap(0, us.at[1 - me_y], row_u)
     ask_u.start()
-    arrived(2)
-    arrived(3)
-    moves[10].start()
-    moves[11].start()
     arrived(6)
     arrived(7)
     moves[12].start()
@@ -517,7 +519,7 @@
         low = roll(cross[64:], 64)
         gw_v[k] = cross[:64] + jnp.where(lane64 < 64, low, -low)
 
-    @pl.loop(0, CHUNKS - 1)
+    @pl.loop(0, EARLY)
     def _(h):
         wait_pencil(rsem.at[12 + h], r3, h)
         y_inverse(r3, pl.multiple_of(h * HC, HC), HC, ly)
@@ -533,30 +535,34 @@
     wait_dp(ssem.at[17], gr)
     for h in range(CHUNKS):
         wait_pencil(ssem.at[12 + h], s3, h)
-    wait_pencil(rsem.at[12 + CHUNKS - 1], r3, CHUNKS - 1)
+    for h in range(EARLY, CHUNKS):
+        wait_pencil(rsem.at[12 + h], r3, h)
 
 
 def last_kernel(
     r_ref, sp, gw_v, tt_ref, zt_ref, done, out_hbm, gw_hbm, ly, vy, out_v, osem,
 ):
-    every, rest = slice(None), CH - HC
+    every = slice(None)
     copies = [
         pltpu.make_async_copy(
-            done.at[x], out_hbm.at[0, x, every, every, pl.ds(0, rest)], osem.at[x]
+            done.at[x], out_hbm.at[0, x, every, every, pl.ds(0, EARLY * HC)], osem.at[x]
         )
         for x in range(4)
     ]
     copies.append(pltpu.make_async_copy(gw_v, gw_hbm.at[0, 0], osem.at[4]))
     for copy in copies:
         copy.start()
-    y_inverse(r_ref, rest, HC, ly)
-    finish(grid_modes(ly, vy, tt_ref), zt_ref, sp, out_v, pl.ds(rest, HC), pl.ds(0, HC))
-    copies.append(
-        pltpu.make_async_copy(
-            out_v, out_hbm.at[0, every, every, every, pl.ds(rest, HC)], osem.at[5]
-        )
-    )
-    copies[5].start()
+    for h in range(EARLY, CHUNKS):
+        i = h - EARLY
+        y_inverse(r_ref, h * HC, HC, ly.at[i])
+        lhs = grid_modes(ly.at[i], vy.at[i], tt_ref)
+        finish(lhs, zt_ref, sp, out_v.at[i], pl.ds(h * HC, HC), every)
+        copies.append(
+            pltpu.make_async_copy(
+                out_v.at[i], out_hbm.at[0, every, every, every, pl.ds(h * HC, HC)], osem.at[5 + i]
+            )
+        )
+        copies[5 + i].start()
     for copy in copies:
         copy.wait()
 
@@ -583,7 +589,7 @@
             pltpu.VMEM((MZ, CH, 2 * CH), F32),
             line_t,
             line_t,
-            pltpu.VMEM((4, 8, 8, CH - HC, NZ), BF16),
+            pltpu.VMEM((4, 8, 8, EARLY * HC, NZ), BF16),
         ),
         in_specs=[any_spec] * 8,
         out_specs=[vmem_spec] * 6,
@@ -617,7 +623,7 @@
             pltpu.SemaphoreType.DMA((4,)),
         ],
         compiler_params=pltpu.CompilerParams(
-            collective_id=0, has_side_effects=True, vmem_limit_bytes=57_700_000
+            collective_id=0, has_side_effects=True, vmem_limit_bytes=58_700_000
         ),
         name="layer",
     )(field.reshape((1,) + grid), cotangent.reshape((1,) + grid), w_spec, w_local, t, tt, zf, zt)
@@ -630,10 +636,10 @@
         in_specs=[vmem_spec] * 6,
         out_specs=[any_spec] * 2,
         scratch_shapes=[
-            pltpu.VMEM((8 * HC, 256), BF16),
-            pltpu.VMEM((8 * HC, 1024), BF16),
-            pltpu.VMEM((4, 8, 8, HC, NZ), BF16),
-            pltpu.SemaphoreType.DMA((6,)),
+            pltpu.VMEM((CHUNKS - EARLY, 8 * HC, 256), BF16),
+            pltpu.VMEM((CHUNKS - EARLY, 8 * HC, 1024), BF16),
+            pltpu.VMEM((CHUNKS - EARLY, 4, 8, 8, HC, NZ), BF16),
+            pltpu.SemaphoreType.DMA((5 + CHUNKS - EARLY,)),
         ],
         compiler_params=pltpu.CompilerParams(vmem_limit_bytes=20 * 1024 * 1024),
         name="last",

time: 66.5 us -> 66.5 us (level)
  no operation moved by 1% of the time
where the time goes in v9:
time: 66.5 us; the launch traced here: 66 us
  Pallas kernels  65.4 us (98%)
    pallas_call x1, Pallas kernels, body(): pl.pallas_call(kernel, out_shape=(pencil_buf, grid_b16, pltpu.VMEM((MZ, C...  62.6 us
    pallas_call x1, Pallas kernels, body(): pl.pallas_call(last_kernel, out_shape=(jax.ShapeDtypeStruct((1,) + grid,...  2.83 us

profile of v9, /device:TPU:8, one launch (start us, length us, event | category | flops | bytes accessed | tf_op | source)
XLA Modules:
  0.0 66.0 jit_solution(13923121764166046203)
XLA Ops:
  0.6 62.6 %layer.1 = (bf16[16,64,128]{2,1,0:T(8,128)(2,1)S(1)}, bf16[4,8,8,64,128]{4,3,2,1,0:T(8,128)(2,1)S(1)}, f32[16,64,128]{2,1,0:T(8,128)S(1)}, bf16[256,1024]{1,0:T(...) custom-call(bf16[1,4,8,8,64,128]{5,4,3,2,1,0:T(8,128)(2,1)} %bitcast.3, ...), custom_call_target="tpu_custom_call" | custom-call | tf_op jit(solution)/shard_map/layer/pallas_call | solution.py:584
  63.2 2.8 %last.1 = (bf16[1,4,8,8,64,128]{5,4,3,2,1,0:T(8,128)(2,1)}, f32[1,1,16,64,128]{4,3,2,1,0:T(8,128)}) custom-call(bf16[16,64,128]{2,1,0:T(8,128)(2,1)S(1)} %get-tuple-element.10.r_ref, bf16[4,8,8,64,128]{4,3,2,1,0:T(8,128)(2,1)S(1)} %get-tuple-element.11.sp, f32[16,64,128]{2,1,0:T(8,128)S(1)} %get-tuple-element.12.gw_v, ...), custom_call_target="tpu_custom_call" | custom-call | tf_op jit(solution)/shard_map/last/pallas_call | solution.py:630
